TPU v7x, 128 devices: a whole 4x4x4 slice. The times are simulated.
128 devices in a mesh: row: 4 (over z), col: 2 (over y_lo), ex: 16 (over x, y_hi, core).
Axes of the slice: x: 4, y: 4 (y_hi: 2, y_lo: 2; y = y_hi * 2 + y_lo), z: 4, core: 2. Of those that a mesh axis runs over, the one named last changes fastest.
Arguments:
- train_in: bfloat16 [8192, 8192], P('ex', 'row'), may hold values from -6 to 6
- train_out: bfloat16 [8192, 8192], P('ex', 'col'), may hold values from -0.0047912598 to 0.0047912598
- query_in: bfloat16 [512, 8192], P('ex', 'row'), may hold values from -6 to 6
- query_out: bfloat16 [512, 8192], P('ex', 'col'), may hold values from -0.023925781 to 0.023925781
- query_ids: int32 [512], P('ex'), may hold values from 0 to 1
- in_basis: bfloat16 [8, 1024, 1024], P('row'), may hold values from -1 to 1, as said below
- out_basis: bfloat16 [8, 1024, 1024], P('col'), may hold values from -1 to 1, as said below
- level_table: float32 [64, 64], replicated, may hold values from 0.5 to 8
- in_level: int32 [8192], P('row'), may hold values from 0 to 63
- out_level: int32 [8192], P('col'), may hold values from 0 to 63
- lengths: int32 [4], replicated, may hold values from 1 to 4096, 8192 in all
Outputs:
- token_scores: float32 [2, 8192], P(None, 'ex')
- example_scores: float32 [2, 4], replicated
Inputs may be any that keep to these rules, and one draw needn't show every extreme that they name: `in_basis`: each block is an orthogonal matrix rounded to bfloat16. `out_basis`: each block is an orthogonal matrix rounded to bfloat16. `lengths`: the counts sum to 8192.
All inputs are finite; a program needn't handle non-finite values.
Results may differ from a plain program's by a relative error of at most 0.018.
Values may be sent and summed in bfloat16 or wider, within the bound.
No kernel may reach another device: no remote copies, remote signals or barrier semaphores. Data moves between devices by JAX's collectives and lax.ppermute only.
A program may use at most 192 MiB of HBM per device.

v0:
```python
import math

import jax
import jax.numpy as jnp
from jax import lax
from jax.sharding import PartitionSpec as P

QUERIES = 2


DAMPING = 0.1


def sent_together(arrays, axis, dim, along):
    widths = [math.prod(a.shape[along:]) for a in arrays]
    both = jnp.concatenate(
        [a.reshape(*a.shape[:along], w) for a, w in zip(arrays, widths)], axis=along
    )
    whole = lax.all_gather(both, axis, axis=dim, tiled=True)
    parts = jnp.split(whole, [sum(widths[:k]) for k in range(1, len(widths))], axis=along)
    return tuple((b.reshape(*whole.shape[:along], *a.shape[along:]) for a, b in zip(arrays, parts)))


def sent_to_all(shard, axis):
    size = lax.axis_size(axis)
    return lax.all_to_all(
        jnp.broadcast_to(shard[None], (size, *shard.shape)), axis, 0, 0, tiled=True
    )


def taken_together(shard, axis):
    everything = sent_to_all(shard, axis)
    return jnp.sum(everything, axis=0)


def body(
    train_in,
    train_out,
    query_in,
    query_out,
    query_ids,
    in_basis,
    out_basis,
    level_table,
    in_level,
    out_level,
    lengths,
):
    highest = lax.Precision.HIGHEST
    ex_count = lax.axis_size("ex")
    ex_index = lax.axis_index("ex")
    in_sub = in_basis.shape[0]
    out_sub = out_basis.shape[0]
    width = in_basis.shape[1]
    per_query = in_sub * out_sub
    owned = QUERIES * per_query // ex_count
    block_ids = ex_index * owned + jnp.arange(owned, dtype=jnp.int32)
    query_of = block_ids % QUERIES
    pair_of = block_ids // QUERIES
    out_of = pair_of // in_sub
    in_of = pair_of % in_sub
    out_own = jnp.take(out_basis, out_of, axis=0)
    in_own = jnp.take(in_basis, in_of, axis=0)
    query_code = query_of.astype(jnp.float32)
    piece_in, piece_out, piece_ids = sent_together(
        (query_in, query_out, query_ids.astype(jnp.bfloat16)), "ex", 0, 1
    )
    count = piece_in.shape[0]
    chosen_in = jnp.take(piece_in.reshape(count, in_sub, width), in_of, axis=1)
    chosen_out = jnp.take(piece_out.reshape(count, out_sub, width), out_of, axis=1)
    weights = (piece_ids.astype(jnp.float32)[:, None] == query_code[None, :]).astype(jnp.bfloat16)
    chosen_out = chosen_out * weights[:, :, None]
    grad_own = jnp.einsum("mka,mkb->kab", chosen_out, chosen_in, preferred_element_type=jnp.float32)
    grad_own = grad_own.astype(jnp.bfloat16)
    half = jnp.einsum("kab,kac->kbc", out_own, grad_own, preferred_element_type=jnp.float32).astype(
        jnp.bfloat16
    )
    rotated = jnp.einsum("kbc,kcd->kbd", half, in_own, preferred_element_type=jnp.float32)
    levels = jnp.arange(level_table.shape[0], dtype=jnp.int32)
    out_levels = jnp.take(out_level.reshape(out_sub, width), out_of, axis=0)
    in_levels = jnp.take(in_level.reshape(in_sub, width), in_of, axis=0)
    out_onehot = (out_levels[:, :, None] == levels[None, None, :]).astype(jnp.float32)
    in_onehot = (in_levels[:, :, None] == levels[None, None, :]).astype(jnp.float32)
    partway = jnp.einsum("kbl,lm->kbm", out_onehot, level_table, precision=highest)
    eigen = jnp.einsum("kbm,kdm->kbd", partway, in_onehot, precision=highest)
    damped = (rotated / (eigen + DAMPING)).astype(jnp.bfloat16)
    back = jnp.einsum("kbd,kcd->kbc", damped, in_own, preferred_element_type=jnp.float32).astype(
        jnp.bfloat16
    )
    precond = jnp.einsum("kab,kbc->kac", out_own, back, preferred_element_type=jnp.float32).astype(
        jnp.bfloat16
    )
    tokens = train_in.shape[0]
    in_split = train_in.reshape(tokens, in_sub, width)
    out_split = train_out.reshape(tokens, out_sub, width)
    query_range = jnp.arange(QUERIES, dtype=jnp.int32)
    piece = lax.all_gather(precond, "ex", axis=0, tiled=True)

    def score_one(step, running):
        pair = step // QUERIES
        matrix = lax.dynamic_index_in_dim(piece, step, 0, keepdims=False)
        acts = lax.dynamic_index_in_dim(in_split, pair % in_sub, 1, keepdims=False)
        grads = lax.dynamic_index_in_dim(out_split, pair // in_sub, 1, keepdims=False)
        image = lax.dot_general(
            acts, matrix, (((1,), (1,)), ((), ())), preferred_element_type=jnp.float32
        )
        values = jnp.sum(image * grads.astype(jnp.float32), axis=1)
        selector = (query_range == step % QUERIES).astype(jnp.float32)
        return running + selector[:, None] * values[None, :]

    token_part = lax.fori_loop(
        0, piece.shape[0], score_one, jnp.zeros((QUERIES, tokens), jnp.float32)
    )
    token_scores = taken_together(token_part, ("row", "col"))
    ends = jnp.cumsum(lengths)
    starts = ends - lengths
    positions = ex_index * tokens + jnp.arange(tokens, dtype=jnp.int32)
    member = (
        (positions[None, :] >= starts[:, None]) & (positions[None, :] < ends[:, None])
    ).astype(jnp.float32)
    local_part = lax.dot_general(token_scores, member, (((1,), (1,)), ((), ())), precision=highest)
    example_scores = taken_together(local_part, "ex")
    return (token_scores, example_scores)


def solution(mesh):
    placed = (
        P("ex", "row"),
        P("ex", "col"),
        P("ex", "row"),
        P("ex", "col"),
        P("ex"),
        P("row", None, None),
        P("col", None, None),
        P(),
        P("row"),
        P("col"),
        P(),
    )
    return jax.shard_map(
        body, mesh=mesh, in_specs=placed, out_specs=(P(None, "ex"), P()), check_vma=False
    )
```

profile of v0, /device:TPU:1, one launch (start us, length us, event | category | flops | bytes accessed | tf_op | source)
XLA Modules:
  0.0 416.8 jit_solution(11040072974099691769)
XLA Ops:
  8.0 1.8 pad_maximum_fusion
  11.9 66.4 %all-gather.4.cloned.1.call-done = bf16[512,6145]{1,0:T(8,128)(2,1)} async-done(((bf16[32,6145]{1,0:T(8,128)(2,1)}), bf16[512,6145]{1,0:T(8,128)(2,1)}) %all-gather.4.cloned.1.call-update) | async-done | bytes 6292496 | tf_op jit(solution)/shard_map/all_gather | solution.py:19
  78.3 4.7 %split.12 = bf16[512,4096]{1,0:T(8,128)(2,1)} slice(bf16[512,6145]{1,0:T(8,128)(2,1)} %all-gather.4.cloned.1.call-done), slice={[0:512], [2048:6144]} | slice | bytes 8388608 | tf_op jit(solution)/shard_map/split | solution.py:20
  83.0 6.5 %copy.58 = bf16[512,4096]{0,1:T(8,128)(2,1)} copy(bf16[512,4096]{1,0:T(8,128)(2,1)} %split.12) | data formatting | bytes 8388608
  93.0 2.6 copy.59
  96.5 5.5 %fusion.17 = bf16[1024,1024]{1,0:T(8,128)(2,1)S(1)} fusion(bf16[4,1024,1024]{2,1,0:T(8,128)(2,1)} %param.19, s32[]{:T(128)} %bitcast.3, pred[]{:T(512)} %bitcast.2, bf16[512,1,1024]{2,0,1:T(8,128)(2,1)S(1)} %copy.46, bf16[512,2,1024]{0,2,1:T(8,128)(2,1)} %bitcast.75, s32[]{:T(128)} %bitcast.12, pred[]{:T(512)} %bitcast.10, bf16[512]{0:T(512)(128)(2,1)S(1)} %fusion.55), kind=kOutput, calls=%fused_computation.19 | convolution fusion | flops 3224371200 | bytes 6294528 | tf_op jit(solution)/shard_map/kab,kac->kbc/dot_general | solution.py:75
  102.1 3.9 fusion.13
  106.0 2.5 divide_convert_fusion
  108.5 8.1 %fusion.22 = bf16[1024,1024]{1,0:T(8,128)(2,1)} fusion(bf16[4,1024,1024]{2,1,0:T(8,128)(2,1)} %param.19, s32[]{:T(128)} %bitcast.3, pred[]{:T(512)} %bitcast.2, bf16[1024,1024]{1,0:T(8,128)(2,1)S(1)} %divide_convert_fusion, bf16[2,1024,1024]{2,1,0:T(8,128)(2,1)} %param.18, s32[]{:T(128)} %bitcast.12, pred[]{:T(512)} %bitcast.10), kind=kOutput, calls=%fused_computation.26 | convolution fusion | flops 4299161600 | bytes 8390656 | tf_op jit(solution)/shard_map/kab,kbc->kac/dot_general | solution.py:90
  116.6 6.7 %copy.49 = bf16[512,4096]{0,1:T(8,128)(2,1)} copy(bf16[512,4096]{1,0:T(8,128)(2,1)} %param.14) | data formatting | bytes 8388608 | tf_op args[1]
  123.4 2.5 copy.43
  126.1 176.4 %all-gather.6.cloned.1.call-done = bf16[16384,1024]{1,0:T(8,128)(2,1)} async-done(((bf16[1024,1024]{1,0:T(8,128)(2,1)}), bf16[16384,1024]{1,0:T(8,128)(2,1)}) %all-gather.6.cloned.1.call-update) | async-done | bytes 33554448 | tf_op jit(solution)/shard_map/all_gather | solution.py:97
  302.5 84.1 %while.23 = (s32[]{:T(128)}, f32[2,512]{1,0:T(2,128)S(1)}, bf16[512,2,1024]{0,2,1:T(8,128)(2,1)}, bf16[16,1024,1024]{2,1,0:T(8,128)(2,1)}, bf16[512,4,1024]{0,2,...) while((s32[]{:T(128)}, f32[2,512]{1,0:T(2,128)S(1)}, ...), condition=%wide.region_2.3_spmd.clone, body=%wide.region_0.2_spmd.clone.sunk | while | flops 1075317248 | bytes 8401917 | solution.py:111
  304.3 3.3 fusion.80
  309.6 3.3 fusion.80
  314.8 3.3 fusion.80
  320.1 3.3 fusion.80
  325.3 3.3 fusion.80
  330.6 3.3 fusion.80
  335.8 3.3 fusion.80
  341.1 3.3 fusion.80
  346.4 3.3 fusion.80
  351.6 3.3 fusion.80
  356.9 3.3 fusion.80
  362.1 3.3 fusion.80
  367.4 3.3 fusion.80
  372.6 3.3 fusion.80
  377.9 3.3 fusion.80
  383.1 3.3 fusion.80
  387.2 4.2 %all-to-all-start = ((f32[8,2,512]{2,1,0:T(2,128)}), f32[8,2,512]{2,1,0:T(2,128)S(1)}, u32[]{:S(2)}, u32[]{:S(2)}) async-start(f32[8,2,512]{2,1,0:T(2,128)} %broadcast_in_dim.102), calls=%async_computation | async-start | bytes 65536 | tf_op jit(solution)/shard_map/all_to_all | solution.py:26
  391.3 5.1 %all-to-all-done = f32[8,2,512]{2,1,0:T(2,128)S(1)} async-done(((f32[8,2,512]{2,1,0:T(2,128)}), f32[8,2,512]{2,1,0:T(2,128)S(1)}, u32[]{:S(2)}, u32[]{:S(2)}) %all-to-all-start) | async-done | bytes 32800 | tf_op jit(solution)/shard_map/all_to_all | solution.py:26
  396.7 12.6 %all_to_all.10 = f32[16,2,4]{2,1,0:T(2,128)S(1)} all-to-all(f32[16,2,4]{2,1,0:T(2,128)S(1)} %broadcast_in_dim.103), channel_id=1, replica_groups=mesh['row'=4,'col'=2,'ex'=16] {'ex'}, dimensions={0} | all-to-all | bytes 1024 | tf_op jit(solution)/shard_map/all_to_all | solution.py:26
  (99 shorter events, 39.6 us)
Async XLA Ops:
  7.2 4.2 %copy-start = (f32[64,64]{1,0:T(8,128)S(1)}, f32[64,64]{1,0:T(8,128)}, u32[]{:S(2)}) copy-start(f32[64,64]{1,0:T(8,128)} %param.20) | copy-start | bytes 49156
  7.2 71.2 %all-gather.4.cloned.1.call-start = ((), (), s32[]{:S(2)}) async-start(), calls=%async_computation.2 | async-start | bytes 6823936 | tf_op jit(solution)/shard_map/all_gather | solution.py:19
  9.8 292.7 %all-gather.6.cloned.1.call-start = ((), (), s32[]{:S(2)}) async-start(), calls=%async_computation.3 | async-start | bytes 35651584 | tf_op jit(solution)/shard_map/all_gather | solution.py:97
  91.4 1.6 slice-start
  116.6 6.7 %copy-start.2 = (bf16[512,2048]{1,0:T(8,128)(2,1)S(1)}, bf16[512,2048]{1,0:T(8,128)(2,1)}, u32[]{:S(2)}) copy-start(bf16[512,2048]{1,0:T(8,128)(2,1)} %param.13) | copy-start | bytes 6291460
  123.4 2.5 copy-start.4
  386.5 23.4 %copy-start.1 = (f32[64,64]{1,0:T(8,128)S(1)}, f32[64,64]{1,0:T(8,128)}, u32[]{:S(2)}) copy-start(f32[64,64]{1,0:T(8,128)} %param.20) | copy-start | bytes 49156
  387.2 9.3 %all-to-all-start = ((f32[8,2,512]{2,1,0:T(2,128)}), f32[8,2,512]{2,1,0:T(2,128)S(1)}, u32[]{:S(2)}, u32[]{:S(2)}) async-start(f32[8,2,512]{2,1,0:T(2,128)} %broadcast_in_dim.102), calls=%async_computation | async-start | bytes 65536 | tf_op jit(solution)/shard_map/all_to_all | solution.py:26
  396.5 13.5 %copy-start.3 = (f32[2,512]{1,0:T(2,128)}, f32[2,512]{1,0:T(2,128)S(1)}, u32[]{:S(2)}) copy-start(f32[2,512]{1,0:T(2,128)S(1)} %reduce_sum.35) | copy-start | bytes 12292
Sparse Core Ops, SparseCore 0:
  10.4 67.9 all-gather.3
  116.7 185.6 all-gather.5
where the time goes:
time: 418 us; the launch traced here: 417 us
  waiting for transfers between devices  248 us (59%)
  matrix products  73.6 us (18%)
  local copies, waits for them, and re-layouts  56.6 us (14%)
  between operations  14.2 us (3%)
  blocking collectives  12.6 us (3%)
  other arithmetic  6.94 us (2%)
  starting transfers between devices  4.25 us (1%)
    all_gather x1, waiting for transfers between devices, body(): piece = lax.all_gather(precond, 'ex', axis=0, tiled=True)  176 us
    all_gather x1, waiting for transfers between devices, sent_together(): whole = lax.all_gather(both, axis, axis=dim, tiled=True)  66.4 us
    dot_general x16, matrix products, score_one(): lax.dot_general(acts, matrix, (((1,), (1,)), ((), ())), preferred_element...  52.8 us
    dynamic_slice x32, local copies, waits for them, and re-layouts, score_one(): lax.dynamic_index_in_dim(out_split, pair // in_sub, 1, keepdims=False)  29.2 us
    unnamed x14, local copies, waits for them, and re-layouts  18.3 us
    all_to_all x1, blocking collectives, sent_to_all(): lax.all_to_all(jnp.broadcast_to(shard[None], (size, *shard.shape)), axis,...  12.6 us
  transfers between devices with their start and end apart: 3, of which 3 were waited for; matrix products, arithmetic and copies ran while one was open for 3% of the time, Pallas kernels for 0%

commit v1 on v0

v1 whole, which is shorter than its diff:
```python
import jax
import jax.numpy as jnp
from jax import lax
from jax.experimental import pallas as pl
from jax.experimental.pallas import tpu as pltpu
from jax.sharding import PartitionSpec as P


QUERIES = 2
DAMPING = 0.1
LANES = 128
BF = jnp.bfloat16
F32 = jnp.float32
UNREAD = pl.BlockSpec(memory_space=pl.ANY)


def vmem_limit(mib):
    return pltpu.CompilerParams(vmem_limit_bytes=mib * 2**20)


def turned_train(train_out, train_in, out_basis, in_basis, core, after=()):
    tokens = train_in.shape[0]
    width = in_basis.shape[1]

    def kernel(core_ref, out_ref, in_ref, outer_ref, inner_ref, *refs):
        away_ref, own_ref, acts_ref = refs[-3:]
        step = pl.program_id(0)

        @pl.when(step < 4)
        def _():
            turned = jnp.dot(out_ref[...], outer_ref[0], preferred_element_type=F32).astype(BF)

            @pl.when(step < 2)
            def _():
                away_ref[0] = turned

            @pl.when(step >= 2)
            def _():
                own_ref[0] = turned

        @pl.when(step >= 4)
        def _():
            acts_ref[0] = jnp.dot(
                in_ref[...], inner_ref[0], preferred_element_type=F32
            ).astype(BF)

    def outer(n, s):
        n = jnp.minimum(n, 3)
        return jnp.where(n < 2, (1 - s[0]) * 2 + n, s[0] * 2 + n - 2)

    def inner(n, s):
        return jnp.where(n < 5, s[0], 1 - s[0])

    def result(first):
        return pl.BlockSpec(
            (1, tokens, width), lambda n, s: (jnp.clip(n - first, 0, 1), 0, 0)
        )

    shape = jax.ShapeDtypeStruct((2, tokens, width), BF)
    return pl.pallas_call(
        kernel,
        grid_spec=pltpu.PrefetchScalarGridSpec(
            num_scalar_prefetch=1,
            grid=(6,),
            in_specs=[
                pl.BlockSpec((tokens, width), lambda n, s: (0, outer(n, s))),
                pl.BlockSpec((tokens, width), lambda n, s: (0, inner(n, s))),
                pl.BlockSpec((1, width, width), lambda n, s: (outer(n, s), 0, 0)),
                pl.BlockSpec((1, width, width), lambda n, s: (inner(n, s), 0, 0)),
            ]
            + [UNREAD] * len(after),
            out_specs=(result(0), result(2), result(4)),
        ),
        out_shape=(shape,) * 3,
        cost_estimate=pl.CostEstimate(
            flops=12 * tokens * width * width,
            bytes_accessed=12 * (2 * tokens * width + width * width),
            transcendentals=0,
        ),
        compiler_params=vmem_limit(60),
        name="turned_train",
    )(core[None], train_out, train_in, out_basis, in_basis, *after)


def level_picks(levels, ref):
    row = lax.broadcasted_iota(jnp.int32, (levels, ref.shape[1]), 0)
    return jnp.where(row == ref[...], 1.0, 0.0).astype(BF)


def inverse_sides(level_table, in_levels, after=()):
    levels = level_table.shape[0]
    inputs = in_levels.shape[1]

    def kernel(table_ref, in_ref, *refs):
        table = 1.0 / (table_ref[...] + DAMPING)
        coarse = table.astype(BF)
        fine = (table - coarse.astype(F32)).astype(BF)
        chosen = level_picks(levels, in_ref)
        for n, part in enumerate((coarse, fine)):
            side = jnp.dot(part, chosen, preferred_element_type=F32)
            refs[-1][:, n * levels : (n + 1) * levels] = side.T.astype(BF)

    vmem = pl.BlockSpec(memory_space=pltpu.VMEM)
    return pl.pallas_call(
        kernel,
        in_specs=[vmem, vmem] + [UNREAD] * len(after),
        out_specs=vmem,
        out_shape=jax.ShapeDtypeStruct((inputs, 2 * levels), BF),
        compiler_params=vmem_limit(16),
        name="inverse_sides",
    )(level_table, in_levels, *after)


def gathered(pieces, split):
    rows, columns = pieces[0].shape
    count = len(pieces)

    def kernel(*refs):
        for n in range(count):
            here = slice(n * rows, (n + 1) * rows)
            refs[count][here] = refs[n][:, :split]
            refs[count + 1][here] = refs[n][:, split:]

    shapes = [(count * rows, w) for w in (split, columns - split)]
    return pl.pallas_call(
        kernel,
        grid=(1,),
        in_specs=[pl.BlockSpec((rows, columns), lambda n: (0, 0))] * count,
        out_specs=[pl.BlockSpec(shape, lambda n: (0, 0)) for shape in shapes],
        out_shape=[jax.ShapeDtypeStruct(shape, BF) for shape in shapes],
        compiler_params=vmem_limit(60),
        name="gathered",
    )(*pieces)


def parcels(query_in, query_out, query_ids, core):
    few, inner = query_in.shape
    outer = query_out.shape[1]
    width, half = inner // 2, outer // 2

    def kernel(core_ref, ids_ref, in_ref, out_ref, keep_ref, send_ref):
        row = lax.broadcasted_iota(jnp.int32, (few, LANES), 0)
        codes = jnp.zeros((few, LANES), F32)
        for n in range(few):
            codes = jnp.where(row == n, ids_ref[n].astype(F32), codes)
        codes = codes.astype(BF)

        def fill(ref, which):
            ref[:, :width] = in_ref[:, which * width : (which + 1) * width]
            ref[:, width : width + half] = out_ref[:, which * half : (which + 1) * half]
            ref[:, width + half :] = codes

        @pl.when(core_ref[0] == 0)
        def _():
            fill(keep_ref, 0)
            fill(send_ref, 1)

        @pl.when(core_ref[0] == 1)
        def _():
            fill(keep_ref, 1)
            fill(send_ref, 0)

    shape = jax.ShapeDtypeStruct((few, width + half + LANES), BF)
    smem = pl.BlockSpec(memory_space=pltpu.SMEM)
    return pl.pallas_call(
        kernel,
        grid=(1,),
        in_specs=[
            smem,
            smem,
            pl.BlockSpec((few, inner), lambda n: (0, 0)),
            pl.BlockSpec((few, outer), lambda n: (0, 0)),
        ],
        out_specs=(pl.BlockSpec(shape.shape, lambda n: (0, 0)),) * 2,
        out_shape=(shape, shape),
        compiler_params=vmem_limit(60),
        name="parcels",
    )(core[None], query_ids, query_in, query_out)


def pooled(kept, got, core, width):
    few, total = kept.shape

    def kernel(core_ref, kept_ref, got_ref, in_ref, outs_ref):
        def fill(ref, at):
            rows = slice(at, at + few)
            in_ref[rows] = ref[:, :width]
            outs_ref[rows, :width] = ref[:, width : 2 * width]
            outs_ref[rows, width : width + LANES] = ref[:, total - LANES :]
            outs_ref[rows, width + LANES :] = ref[:, 2 * width : 3 * width]

        @pl.when(core_ref[0] == 0)
        def _():
            fill(kept_ref, 0)
            fill(got_ref, few)

        @pl.when(core_ref[0] == 1)
        def _():
            fill(got_ref, 0)
            fill(kept_ref, few)

    smem = pl.BlockSpec(memory_space=pltpu.SMEM)
    shapes = [(2 * few, w) for w in (width, total - width)]
    return pl.pallas_call(
        kernel,
        grid=(1,),
        in_specs=[smem] + [pl.BlockSpec((few, total), lambda n: (0, 0))] * 2,
        out_specs=[pl.BlockSpec(shape, lambda n: (0, 0)) for shape in shapes],
        out_shape=[jax.ShapeDtypeStruct(shape, BF) for shape in shapes],
        compiler_params=vmem_limit(60),
        name="pooled",
    )(core[None], kept, got)


def rotate_turned(pieces, basis, which, after=(), strip=1024):
    rows = pieces[0].shape[0]
    width = basis.shape[1]
    count = len(pieces)

    def kernel(start_ref, *refs):
        basis_ref, out_ref = refs[count], refs[-1]
        for n in range(count):
            turned = jnp.dot(refs[n][...], basis_ref[0], preferred_element_type=F32)
            out_ref[:, n * rows : (n + 1) * rows] = turned.T.astype(BF)

    return pl.pallas_call(
        kernel,
        grid_spec=pltpu.PrefetchScalarGridSpec(
            num_scalar_prefetch=1,
            grid=(width // strip,),
            in_specs=[pl.BlockSpec((rows, width), lambda n, s: (0, 0))] * count
            + [pl.BlockSpec((1, width, strip), lambda n, s: (0, 0, n))]
            + [UNREAD] * len(after),
            out_specs=pl.BlockSpec((strip, rows * count), lambda n, s: (n, 0)),
        ),
        out_shape=jax.ShapeDtypeStruct((width, rows * count), BF),
        cost_estimate=pl.CostEstimate(
            flops=2 * count * rows * width * width,
            bytes_accessed=2 * (2 * count * rows * width + width * width),
            transcendentals=0,
        ),
        compiler_params=vmem_limit(20),
        name="rotate_turned",
    )(which[None], *pieces, basis, *after)


def spread_out(pieces, coded, basis, which, unit, after=()):
    width = basis.shape[1]
    count, rows = len(pieces), pieces[0].shape[0]
    operands = list(pieces) + ([] if pieces is coded else list(coded))

    def kernel(start_ref, *refs):
        basis_ref, out_ref = refs[len(operands)], refs[-1]
        for y in range(count):
            turned = jnp.dot(refs[y][:, :width], basis_ref[0], preferred_element_type=F32)
            codes = refs[y if pieces is coded else count + y]
            for x in range(rows // unit):
                here = slice(x * unit, (x + 1) * unit)
                code = codes[here, width : width + 1].astype(F32)
                at = (x * count + y) * unit
                for q in range(QUERIES):
                    out_ref[q, at : at + unit] = jnp.where(
                        code == float(q), turned[here], 0.0
                    ).astype(BF)

    return pl.pallas_call(
        kernel,
        grid_spec=pltpu.PrefetchScalarGridSpec(
            num_scalar_prefetch=1,
            grid=(1,),
            in_specs=[pl.BlockSpec(p.shape, lambda n, s: (0, 0)) for p in operands]
            + [pl.BlockSpec((1, width, width), lambda n, s: (0, 0, 0))]
            + [UNREAD] * len(after),
            out_specs=pl.BlockSpec((QUERIES, count * rows, width), lambda n, s: (0, 0, 0)),
        ),
        out_shape=jax.ShapeDtypeStruct((QUERIES, count * rows, width), BF),
        cost_estimate=pl.CostEstimate(
            flops=2 * count * rows * width * width,
            bytes_accessed=2 * (3 * count * rows * width + width * width),
            transcendentals=0,
        ),
        compiler_params=vmem_limit(20),
        name="spread_out",
    )(which[None], *operands, basis, *after)


def score_block(
    turned, spread, sides, out_levels, acts, grads, running, block, strip=512, rows=256
):
    width, qtokens = turned[0].shape
    parts, tokens = acts[0].shape[:2]
    total_shape = (QUERIES, 2 * tokens, LANES)
    strips = width // strip

    levels = sides.shape[1] // 2

    def kernel(t0, t1, spread_ref, sides_ref, levels_ref, a0, a1, g0, g1, *refs):
        out_ref, scratch, inverse_ref = refs[-3:]

        @pl.when(pl.program_id(0) == 0)
        def _():
            out_ref[...] = jnp.zeros(total_shape, F32) if running is None else refs[0][...]

        chosen = level_picks(levels, levels_ref)
        chosen = jnp.concatenate([chosen, chosen])
        for top in range(0, parts * width, rows):
            at = slice(top, top + rows)
            inverse_ref[at] = jnp.dot(sides_ref[at], chosen, preferred_element_type=F32)

        for q in range(QUERIES):
            for p, t in enumerate((t0, t1)):
                for top in range(0, width, rows):
                    at = slice(p * width + top, p * width + top + rows)
                    piece = jnp.dot(t[top : top + rows], spread_ref[q], preferred_element_type=F32)
                    scratch[at] = (piece * inverse_ref[at]).astype(BF)
            for side, (a, g) in enumerate(((a0, g0), (a1, g1))):
                for top in range(0, tokens, rows):
                    image = None
                    for p in range(parts):
                        term = jnp.dot(
                            a[p if side == 0 else 1 - p, top : top + rows],
                            scratch[p * width : (p + 1) * width],
                            preferred_element_type=F32,
                        )
                        image = term if image is None else image + term
                    terms = image * g[0, top : top + rows].astype(F32)
                    total = terms[:, :LANES]
                    for lane in range(LANES, strip, LANES):
                        total = total + terms[:, lane : lane + LANES]
                    at = side * tokens + top
                    out_ref[q, at : at + rows] += total

    once = pl.Buffered(1)
    whole = pl.BlockSpec(acts[0].shape, lambda n: (0, 0, 0), pipeline_mode=once)
    turned_spec = pl.BlockSpec((width, qtokens), lambda n: (0, 0), pipeline_mode=once)
    strip_spec = pl.BlockSpec((1, tokens, strip), lambda n: (block, 0, n))
    run_spec = pl.BlockSpec(total_shape, lambda n: (0, 0, 0), pipeline_mode=once)
    flops = 2 * QUERIES * parts * width * width * (qtokens + 2 * tokens)
    return pl.pallas_call(
        kernel,
        grid=(strips,),
        in_specs=[
            turned_spec,
            turned_spec,
            pl.BlockSpec((QUERIES, qtokens, strip), lambda n: (0, 0, n)),
            pl.BlockSpec(sides.shape, lambda n: (0, 0), pipeline_mode=once),
            pl.BlockSpec((1, strip), lambda n: (0, block * strips + n)),
            whole,
            whole,
            strip_spec,
            strip_spec,
        ]
        + ([] if running is None else [run_spec]),
        out_specs=pl.BlockSpec(total_shape, lambda n: (0, 0, 0)),
        out_shape=jax.ShapeDtypeStruct(total_shape, F32),
        scratch_shapes=[
            pltpu.VMEM((parts * width, strip), BF),
            pltpu.VMEM((parts * width, strip), F32),
        ],
        cost_estimate=pl.CostEstimate(flops=flops, bytes_accessed=16 * 2**20, transcendentals=0),
        compiler_params=vmem_limit(32),
        name="score_block",
    )(*turned, spread, sides, out_levels, *acts, *grads, *([] if running is None else [running]))


def body(
    train_in,
    train_out,
    query_in,
    query_out,
    query_ids,
    in_basis,
    out_basis,
    level_table,
    in_level,
    out_level,
    lengths,
):
    ex_count = lax.axis_size("ex")
    ex_index = lax.axis_index("ex")
    core = ex_index % 2
    in_sub, width = in_basis.shape[0], in_basis.shape[1]
    out_sub = out_basis.shape[0]
    half = out_sub // 2
    tokens = train_in.shape[0]
    few = query_in.shape[0]
    hops = ex_count // 4

    def to_core(a):
        return lax.ppermute(a, "ex", [(i, i ^ 1) for i in range(ex_count)])

    def across_y(a):
        return lax.ppermute(a, "ex", [(i, i ^ 2) for i in range(ex_count)])

    def across_y_and_col(a):
        count = lax.axis_size("col") * ex_count
        return lax.ppermute(a, ("col", "ex"), [(i, i ^ ex_count ^ 2) for i in range(count)])

    def along_x(a):
        return [a] + [
            lax.ppermute(a, "ex", [(i, (i + 4 * n) % ex_count) for i in range(ex_count)])
            for n in range(1, hops)
        ]

    kept, sent = parcels(query_in, query_out, query_ids, core)
    near_in, near_out = pooled(kept, to_core(sent), core, width)
    near_in_y = across_y_and_col(near_in)
    column = jnp.concatenate([near_in, near_in_y])
    row = along_x(near_out)
    rows = gathered(row, width + LANES)
    grads_away, grads_own, acts_own = turned_train(
        train_out, train_in, out_basis, in_basis, core, (near_in,)
    )
    first_pieces, second_pieces = ([r, across_y(r)] for r in rows)
    in_pieces = along_x(column)
    grads_other = to_core(grads_away)
    acts_other = to_core(acts_own)

    in_levels = in_level.reshape(in_sub, width)
    in_levels = jnp.concatenate(
        [lax.dynamic_slice_in_dim(in_levels, n, 1) for n in (core, 1 - core)], axis=1
    )
    out_levels = lax.dynamic_slice_in_dim(out_level, core * half * width, half * width)[None]
    sides = inverse_sides(level_table, in_levels, (grads_own,))

    inner = lax.dynamic_slice_in_dim(in_basis, core, 1)
    outers = [lax.dynamic_slice_in_dim(out_basis, core * half + n, 1) for n in range(half)]
    query_own = rotate_turned(in_pieces, inner, core, (sides, first_pieces[1]))
    query_other = to_core(query_own)
    running = None
    for block, pieces in enumerate((first_pieces, second_pieces)):
        spread = spread_out(
            pieces,
            first_pieces,
            outers[block],
            core,
            2 * few,
            () if running is None else (running,),
        )
        running = score_block(
            (query_own, query_other),
            spread,
            sides,
            out_levels,
            (acts_own, acts_other),
            (grads_own, grads_other),
            running,
            block,
        )

    part = jnp.sum(running, axis=2)
    mine, others = part[:, :tokens], part[:, tokens:]
    token_part = mine + to_core(others)

    def sum_over(shard, axes):
        size = lax.axis_size(axes)
        spread = jnp.broadcast_to(shard[None], (size, *shard.shape))
        return jnp.sum(lax.all_to_all(spread, axes, 0, 0, tiled=True), axis=0)

    token_scores = sum_over(token_part, ("row", "col"))
    ends = jnp.cumsum(lengths)
    starts = ends - lengths
    at = ex_index * tokens + jnp.arange(tokens, dtype=jnp.int32)
    member = (at[None, :] >= starts[:, None]) & (at[None, :] < ends[:, None])
    example_part = jnp.sum(jnp.where(member[None], token_scores[:, None, :], 0.0), axis=2)
    example_scores = sum_over(example_part, "ex")
    return (token_scores, example_scores)


def solution(mesh):
    placed = (
        P("ex", "row"),
        P("ex", "col"),
        P("ex", "row"),
        P("ex", "col"),
        P("ex"),
        P("row", None, None),
        P("col", None, None),
        P(),
        P("row"),
        P("col"),
        P(),
    )
    return jax.shard_map(
        body, mesh=mesh, in_specs=placed, out_specs=(P(None, "ex"), P()), check_vma=False
    )
```

time: 418 us -> 139 us (0.33)
  waiting for transfers between devices: 248 us -> 27.2 us
  matrix products: 73.6 us -> 0 us
  Pallas kernels: 0 us -> 60.8 us
  local copies, waits for them, and re-layouts: 56.6 us -> 8.73 us
  starting transfers between devices: 4.25 us -> 26.5 us
  between operations: 14.2 us -> 0.88 us
  other arithmetic: 6.94 us -> 2.54 us
    all_gather x2 -> x0, waiting for transfers between devices: 243 us -> none  [the longest x1 176 us: body(): piece = lax.all_gather(precond, 'ex', axis=0, tiled=True)]
    dot_general x22 -> x0, matrix products: 73.6 us -> none  [the longest x16 52.8 us: score_one(): lax.dot_general(acts, matrix, (((1,), (1,)), ((), ())), preferred_element...]
    pallas_call x0 -> x10, Pallas kernels: none -> 60.8 us  [the longest x2 34.7 us: score_block(): pl.pallas_call(kernel, grid=(strips,), in_specs=[turned_spec, turned_spec...]
    dynamic_slice x32 -> x4, local copies, waits for them, and re-layouts: 29.2 us -> 4.68 us  [the longest x1 2.76 us: body(): lax.dynamic_slice_in_dim(out_basis, core * half + n, 1)]
    ppermute x0 -> x14, waiting for transfers between devices: none -> 22.2 us  [the longest x6 20 us: along_x(): lax.ppermute(a, 'ex', [(i, (i + 4 * n) % ex_count) for i in range(ex_coun...]
    ppermute x0 -> x14, starting transfers between devices: none -> 21.4 us  [the longest x6 12.3 us: along_x(): lax.ppermute(a, 'ex', [(i, (i + 4 * n) % ex_count) for i in range(ex_coun...]
    unnamed x14 -> x37, local copies, waits for them, and re-layouts: 18.3 us -> 3.4 us
    split x3 -> x0, local copies, waits for them, and re-layouts: 6.29 us -> none  [sent_together(): jnp.split(whole, [sum(widths[:k]) for k in range(1, len(widths))], axis=a...]
  transfers between devices with their start and end apart: 3 -> 15, of which waited for: 3 -> 7; matrix products, arithmetic and copies ran while one was open for 3% -> 4% of each run, Pallas kernels for 0% -> 28%
where the time goes in v1:
time: 139 us; the launch traced here: 138 us
  Pallas kernels  60.8 us (44%)
  waiting for transfers between devices  27.2 us (20%)
  starting transfers between devices  26.5 us (19%)
  blocking collectives  11.5 us (8%)
  local copies, waits for them, and re-layouts  8.73 us (6%)
  other arithmetic  2.54 us (2%)
    pallas_call x2, Pallas kernels, score_block(): pl.pallas_call(kernel, grid=(strips,), in_specs=[turned_spec, turned_spec...  34.7 us
    ppermute x6, waiting for transfers between devices, along_x(): lax.ppermute(a, 'ex', [(i, (i + 4 * n) % ex_count) for i in range(ex_coun...  20 us
    pallas_call x1, Pallas kernels, turned_train(): pl.pallas_call(kernel, grid_spec=pltpu.PrefetchScalarGridSpec(num_scalar_...  14.3 us
    ppermute x6, starting transfers between devices, along_x(): lax.ppermute(a, 'ex', [(i, (i + 4 * n) % ex_count) for i in range(ex_coun...  12.3 us
    all_to_all x1, blocking collectives, sum_over(): return jnp.sum(lax.all_to_all(spread, axes, 0, 0, tiled=True), axis=0)  11.5 us
    all_to_all x1, starting transfers between devices, sum_over(): return jnp.sum(lax.all_to_all(spread, axes, 0, 0, tiled=True), axis=0)  5.04 us
    all_to_all x1, waiting for transfers between devices, sum_over(): return jnp.sum(lax.all_to_all(spread, axes, 0, 0, tiled=True), axis=0)  5.03 us
    unnamed x37, local copies, waits for them, and re-layouts  3.4 us
  transfers between devices with their start and end apart: 15, of which 7 were waited for; matrix products, arithmetic and copies ran while one was open for 4% of the time, Pallas kernels for 28%

profile of v1, /device:TPU:1, one launch (start us, length us, event | category | flops | bytes accessed | tf_op | source)
XLA Modules:
  0.0 138.2 jit_solution(7786257501756618821)
XLA Ops:
  0.6 1.8 %parcels.1 = (bf16[32,3200]{1,0:T(8,128)(2,1)}, bf16[32,3200]{1,0:T(8,128)(2,1)}) custom-call(s32[1]{0:T(128)} %bitcast.core_ref.start_ref, s32[32]{0:T(128)} %ids_ref.1, bf16[32,2048]{1,0:T(8,128)(2,1)} %in_ref.2, bf16[32,4096]{1,0:T(8,128)(2,1)} %out_ref.2), custom_call_target="tpu_custom_call" | custom-call | tf_op jit(solution)/shard_map/parcels/pallas_call | solution.py:165
  2.5 1.4 %collective-permute-start = (bf16[32,3200]{1,0:T(8,128)(2,1)}, bf16[32,3200]{1,0:T(8,128)(2,1)S(1)}, u32[]{:S(2)}, u32[]{:S(2)}) collective-permute-start(bf16[32,3200]{1,0:T(8,128)(2,1)} %get-tuple-element.12), channel_id=1, source_target_pairs={{0,1},{1,0},{2,3},{3,2},{4,5},{5,4},{6,7},{7,6},{8,9},{9,8},{10,11... | collective-permute-start | bytes 614408 | tf_op jit(solution)/shard_map/ppermute | solution.py:390
  3.9 1.3 collective-permute-done.got_ref
  5.2 0.7 copy-done.12
  5.8 1.8 %pooled.1 = (bf16[64,1024]{1,0:T(8,128)(2,1)}, bf16[64,2176]{1,0:T(8,128)(2,1)}) custom-call(s32[1]{0:T(128)} %bitcast.core_ref.start_ref, bf16[32,3200]{1,0:T(8,128)(2,1)} %get-tuple-element.11.kept_ref, bf16[32,3200]{1,0:T(8,128)(2,1)} %copy-done.12), custom_call_target="tpu_custom_call" | custom-call | tf_op jit(solution)/shard_map/pooled/pallas_call | solution.py:204
  7.7 2.9 %collective-permute-start.1 = (bf16[64,1024]{1,0:T(8,128)(2,1)}, bf16[64,1024]{1,0:T(8,128)(2,1)S(1)}, u32[]{:S(2)}, u32[]{:S(2)}) collective-permute-start(bf16[64,1024]{1,0:T(8,128)(2,1)} %get-tuple-element.13.refs_0_), channel_id=1, source_target_pairs={{0,18},{1,19},{2,16},{3,17},{4,22},{5,23},{6,20},{7,21},{8,26},{9,... | collective-permute-start | bytes 393224 | tf_op jit(solution)/shard_map/ppermute | solution.py:397
  10.6 14.3 %turned_train.1 = (bf16[2,512,1024]{2,1,0:T(8,128)(2,1)}, bf16[2,512,1024]{2,1,0:T(8,128)(2,1)}, bf16[2,512,1024]{2,1,0:T(8,128)(2,1)}) custom-call(s32[1]{0:T(128)} %bitcast.core_ref.start_ref, bf16[512,4096]{1,0:T(8,128)(2,1)} %out_ref.3, bf16[512,2048]{1,0:T(8,128)(2,1)} %in_ref.3, bf16[4,1024,1024]{2,1,0:T(8,128)(2,1)} %outer_ref.1, ...), custom_call_target="tpu_custom_call" | custom-call | flops 6442450944 | bytes 25165824 | tf_op jit(solution)/shard_map/turned_train/pallas_call | solution.py:60
  24.9 0.7 collective-permute-start.12
  25.6 2.5 %collective-permute-start.7 = (bf16[64,2176]{1,0:T(8,128)(2,1)S(1)}, bf16[64,2176]{1,0:T(8,128)(2,1)S(1)}, u32[]{:S(2)}, u32[]{:S(2)}) collective-permute-start(bf16[64,2176]{1,0:T(8,128)(2,1)S(1)} %copy-done.8), channel_id=1, source_target_pairs={{0,12},{1,13},{2,14},{3,15},{4,0},{5,1},{6,2},{7,3},{8,4},{9,5},{1... | collective-permute-start | bytes 835592 | tf_op jit(solution)/shard_map/ppermute | solution.py:401
  29.3 5.2 %collective-permute-done.7.refs_3_ = bf16[64,2176]{1,0:T(8,128)(2,1)S(1)} collective-permute-done((bf16[64,2176]{1,0:T(8,128)(2,1)S(1)}, bf16[64,2176]{1,0:T(8,128)(2,1)S(1)}, u32[]{:S(2)}, u32[]{:S(2)}) %collective-permute-start.7) | collective-permute-done | bytes 278560 | tf_op jit(solution)/shard_map/ppermute | solution.py:401
  34.4 8.1 %collective-permute-start.4 = (bf16[128,1024]{1,0:T(8,128)(2,1)S(1)}, bf16[128,1024]{1,0:T(8,128)(2,1)S(1)}, u32[]{:S(2)}, u32[]{:S(2)}) collective-permute-start(bf16[128,1024]{1,0:T(8,128)(2,1)S(1)} %constant_dynamic-update-slice_fusion.refs_0_), channel_id=1, source_target_pairs={{0,12},{1,13},{2,14},{3,15},{4,0},{5,1},{6,2},{7,3},{8,4},{9,5},{1... | collective-permute-start | bytes 786440 | tf_op jit(solution)/shard_map/ppermute | solution.py:401
  42.5 1.6 %collective-permute-done.5.refs_1_ = bf16[64,2176]{1,0:T(8,128)(2,1)S(1)} collective-permute-done((bf16[64,2176]{1,0:T(8,128)(2,1)S(1)}, bf16[64,2176]{1,0:T(8,128)(2,1)S(1)}, u32[]{:S(2)}, u32[]{:S(2)}) %collective-permute-start.5) | collective-permute-done | bytes 278560 | tf_op jit(solution)/shard_map/ppermute | solution.py:401
  44.1 0.7 copy-done.11
  44.9 2.3 %gathered.1 = (bf16[256,1152]{1,0:T(8,128)(2,1)}, bf16[256,1024]{1,0:T(8,128)(2,1)}) custom-call(bf16[64,2176]{1,0:T(8,128)(2,1)} %get-tuple-element.15.refs_0_, bf16[64,2176]{1,0:T(8,128)(2,1)} %copy-done.11, bf16[64,2176]{1,0:T(8,128)(2,1)} %copy-done.10, bf16[64,2176]{1,0:T(8,128)(2,1)} %copy-done.9), custom_call_target="tpu_custom_call" | custom-call | tf_op jit(solution)/shard_map/gathered/pallas_call | solution.py:125
  47.5 1.9 %constant_dynamic-slice_fusion.4.refs_4_ = bf16[1,1024,1024]{2,1,0:T(8,128)(2,1)S(1)} fusion(bf16[2,1024,1024]{2,1,0:T(8,128)(2,1)} %inner_ref.1, s32[]{:T(128)S(6)} %select_n.28), kind=kLoop, calls=%fused_computation.11 | loop fusion | bytes 4194308 | tf_op jit(solution)/shard_map/dynamic_slice | solution.py:426
  50.1 0.7 copy-done.4
  50.8 0.8 inverse_sides.1.refs_5_.sides_ref
  51.6 5.8 %collective-permute-done.3.refs_2_ = bf16[128,1024]{1,0:T(8,128)(2,1)S(1)} collective-permute-done((bf16[128,1024]{1,0:T(8,128)(2,1)S(1)}, bf16[128,1024]{1,0:T(8,128)(2,1)S(1)}, u32[]{:S(2)}, u32[]{:S(2)}) %collective-permute-start.3) | collective-permute-done | bytes 262176 | tf_op jit(solution)/shard_map/ppermute | solution.py:401
  57.5 7.4 %collective-permute-done.2.refs_1_ = bf16[128,1024]{1,0:T(8,128)(2,1)S(1)} collective-permute-done((bf16[128,1024]{1,0:T(8,128)(2,1)S(1)}, bf16[128,1024]{1,0:T(8,128)(2,1)S(1)}, u32[]{:S(2)}, u32[]{:S(2)}) %collective-permute-start.2) | collective-permute-done | bytes 262176 | tf_op jit(solution)/shard_map/ppermute | solution.py:401
  64.9 2.4 %rotate_turned.1.t0 = bf16[1024,512]{1,0:T(8,128)(2,1)} custom-call(s32[1]{0:T(128)} %bitcast.core_ref.start_ref, bf16[128,1024]{1,0:T(8,128)(2,1)S(1)} %constant_dynamic-update-slice_fusion.refs_0_, bf16[128,1024]{1,0:T(8,128)(2,1)S(1)} %collective-permute-done.2.refs_1_, bf16[128,1024]{1,0:T(8,128)(2,1)S(1)} %collective-permute-done.3.refs_2_, ...), custom_call_target="tpu_custom_call" | custom-call | flops 1073741824 | bytes 4194304 | tf_op jit(solution)/shard_map/rotate_turned/pallas_call | solution.py:226
  68.0 2.8 %constant_dynamic-slice_fusion = (bf16[1,1024,1024]{2,1,0:T(8,128)(2,1)S(1)}, bf16[1,1024,1024]{2,1,0:T(8,128)(2,1)S(1)}) fusion(bf16[4,1024,1024]{2,1,0:T(8,128)(2,1)} %outer_ref.1, s32[]{:T(128)S(6)} %select_n.31, s32[]{:T(128)S(6)} %select_n.30), kind=kLoop, calls=%fused_computation.7 | loop fusion | bytes 8388616 | tf_op jit(solution)/shard_map/dynamic_slice | solution.py:427
  70.8 2.9 %collective-permute-start.10 = (bf16[256,1024]{1,0:T(8,128)(2,1)S(1)}, bf16[256,1024]{1,0:T(8,128)(2,1)S(1)}, u32[]{:S(2)}, u32[]{:S(2)}) collective-permute-start(bf16[256,1024]{1,0:T(8,128)(2,1)S(1)} %copy-done.3), channel_id=1, source_target_pairs={{0,2},{1,3},{2,0},{3,1},{4,6},{5,7},{6,4},{7,5},{8,10},{9,11},{10,... | collective-permute-start | bytes 1572872 | tf_op jit(solution)/shard_map/ppermute | solution.py:393
  73.7 1.3 spread_out.2.spread_ref
  75.3 17.2 %score_block.2.refs_5_.refs_0_ = f32[2,1024,128]{2,1,0:T(8,128)S(1)} custom-call(bf16[1024,512]{1,0:T(8,128)(2,1)} %rotate_turned.1.t0, bf16[1024,512]{1,0:T(8,128)(2,1)} %collective-permute-done.9.t1, bf16[2,512,1024]{2,1,0:T(8,128)(2,1)S(1)} %spread_out.2.spread_ref, bf16[2048,128]{1,0:T(8,128)(2,1)S(1)} %inverse_sides.1.refs_5_.sides_ref, ...), custom_call_target="tpu_custom_call" | custom-call | flops 12884901888 | bytes 16777216 | tf_op jit(solution)/shard_map/score_block/pallas_call | solution.py:339
  92.5 1.3 spread_out.3.spread_ref
  93.9 17.5 %score_block.3 = f32[2,1024,128]{2,1,0:T(8,128)S(1)} custom-call(bf16[1024,512]{1,0:T(8,128)(2,1)} %rotate_turned.1.t0, bf16[1024,512]{1,0:T(8,128)(2,1)} %collective-permute-done.9.t1, bf16[2,512,1024]{2,1,0:T(8,128)(2,1)S(1)} %spread_out.3.spread_ref, bf16[2048,128]{1,0:T(8,128)(2,1)S(1)} %inverse_sides.1.refs_5_.sides_ref, s32[1,2048]{1,0:T(1,128)S(1)} %bitcast.6, ...), custom_call_target="tpu_custom_call" | custom-call | flops 12884901888 | bytes 16777216 | tf_op jit(solution)/shard_map/score_block/pallas_call | solution.py:339
  111.3 1.0 copy-done.2
  112.3 1.6 %reduce_sum.36 = f32[2,1024]{1,0:T(2,128)S(1)} reduce(f32[2,1024,128]{2,1,0:T(8,128)} %copy-done.2, f32[]{:T(128)} %constant.35.clone.1), dimensions={2}, to_apply=%region_0.1 | reduce | flops 260096 | bytes 1056772 | tf_op jit(solution)/shard_map/reduce_sum | solution.py:451
  114.3 0.9 collective-permute-done.13
  115.8 5.0 %all-to-all-start = ((f32[8,2,512]{2,1,0:T(2,128)}), f32[8,2,512]{2,1,0:T(2,128)S(1)}, u32[]{:S(2)}, u32[]{:S(2)}) async-start(f32[8,2,512]{2,1,0:T(2,128)} %broadcast_in_dim.23), calls=%async_computation | async-start | bytes 65536 | tf_op jit(solution)/shard_map/all_to_all | solution.py:458
  120.9 5.0 %all-to-all-done = f32[8,2,512]{2,1,0:T(2,128)S(1)} async-done(((f32[8,2,512]{2,1,0:T(2,128)}), f32[8,2,512]{2,1,0:T(2,128)S(1)}, u32[]{:S(2)}, u32[]{:S(2)}) %all-to-all-start) | async-done | bytes 32800 | tf_op jit(solution)/shard_map/all_to_all | solution.py:458
  126.1 11.5 %all_to_all.10 = f32[16,2,4]{2,1,0:T(2,128)S(1)} all-to-all(f32[16,2,4]{2,1,0:T(2,128)S(1)} %broadcast_in_dim.34), channel_id=1, replica_groups=mesh['row'=4,'col'=2,'ex'=16] {'ex'}, dimensions={0} | all-to-all | bytes 1024 | tf_op jit(solution)/shard_map/all_to_all | solution.py:458
  (65 shorter events, 5.0 us)
Async XLA Ops:
  2.5 2.7 %collective-permute-start = (bf16[32,3200]{1,0:T(8,128)(2,1)}, bf16[32,3200]{1,0:T(8,128)(2,1)S(1)}, u32[]{:S(2)}, u32[]{:S(2)}) collective-permute-start(bf16[32,3200]{1,0:T(8,128)(2,1)} %get-tuple-element.12), channel_id=1, source_target_pairs={{0,1},{1,0},{2,3},{3,2},{4,5},{5,4},{6,7},{7,6},{8,9},{9,8},{10,11... | collective-permute-start | bytes 614408 | tf_op jit(solution)/shard_map/ppermute | solution.py:390
  7.7 17.9 %copy-start.8 = (bf16[64,2176]{1,0:T(8,128)(2,1)S(1)}, bf16[64,2176]{1,0:T(8,128)(2,1)}, u32[]{:S(2)}) copy-start(bf16[64,2176]{1,0:T(8,128)(2,1)} %get-tuple-element.15.refs_0_) | copy-start | bytes 835588
  7.7 21.6 %copy-start.13 = (bf16[64,1024]{1,0:T(8,128)(2,1)S(1)}, bf16[64,1024]{1,0:T(8,128)(2,1)}, u32[]{:S(2)}) copy-start(bf16[64,1024]{1,0:T(8,128)(2,1)} %get-tuple-element.13.refs_0_) | copy-start | bytes 393220
  7.7 39.8 %copy-start.15 = (s32[2048]{0:T(1024)S(1)}, s32[2048]{0:T(1024)}, u32[]{:S(2)}) copy-start(s32[2048]{0:T(1024)} %param.19) | copy-start | bytes 24580
  7.7 20.9 %collective-permute-start.1 = (bf16[64,1024]{1,0:T(8,128)(2,1)}, bf16[64,1024]{1,0:T(8,128)(2,1)S(1)}, u32[]{:S(2)}, u32[]{:S(2)}) collective-permute-start(bf16[64,1024]{1,0:T(8,128)(2,1)} %get-tuple-element.13.refs_0_), channel_id=1, source_target_pairs={{0,18},{1,19},{2,16},{3,17},{4,22},{5,23},{6,20},{7,21},{8,26},{9,... | collective-permute-start | bytes 393224 | tf_op jit(solution)/shard_map/ppermute | solution.py:397
  24.9 50.1 %collective-permute-start.12 = (bf16[2,512,1024]{2,1,0:T(8,128)(2,1)}, bf16[2,512,1024]{2,1,0:T(8,128)(2,1)}, u32[]{:S(2)}, u32[]{:S(2)}) collective-permute-start(bf16[2,512,1024]{2,1,0:T(8,128)(2,1)} %get-tuple-element.19), channel_id=1, source_target_pairs={{0,1},{1,0},{2,3},{3,2},{4,5},{5,4},{6,7},{7,6},{8,9},{9,8},{10,11... | collective-permute-start | bytes 6291464 | tf_op jit(solution)/shard_map/ppermute | solution.py:390
  25.5 49.5 %collective-permute-start.11 = (bf16[2,512,1024]{2,1,0:T(8,128)(2,1)}, bf16[2,512,1024]{2,1,0:T(8,128)(2,1)}, u32[]{:S(2)}, u32[]{:S(2)}) collective-permute-start(bf16[2,512,1024]{2,1,0:T(8,128)(2,1)} %get-tuple-element.18.a0), channel_id=1, source_target_pairs={{0,1},{1,0},{2,3},{3,2},{4,5},{5,4},{6,7},{7,6},{8,9},{9,8},{10,11... | collective-permute-start | bytes 6291464 | tf_op jit(solution)/shard_map/ppermute | solution.py:390
  25.6 8.8 %collective-permute-start.7 = (bf16[64,2176]{1,0:T(8,128)(2,1)S(1)}, bf16[64,2176]{1,0:T(8,128)(2,1)S(1)}, u32[]{:S(2)}, u32[]{:S(2)}) collective-permute-start(bf16[64,2176]{1,0:T(8,128)(2,1)S(1)} %copy-done.8), channel_id=1, source_target_pairs={{0,12},{1,13},{2,14},{3,15},{4,0},{5,1},{6,2},{7,3},{8,4},{9,5},{1... | collective-permute-start | bytes 835592 | tf_op jit(solution)/shard_map/ppermute | solution.py:401
  28.1 14.4 %collective-permute-start.6 = (bf16[64,2176]{1,0:T(8,128)(2,1)S(1)}, bf16[64,2176]{1,0:T(8,128)(2,1)S(1)}, u32[]{:S(2)}, u32[]{:S(2)}) collective-permute-start(bf16[64,2176]{1,0:T(8,128)(2,1)S(1)} %copy-done.8), channel_id=1, source_target_pairs={{0,8},{1,9},{2,10},{3,11},{4,12},{5,13},{6,14},{7,15},{8,0},{9,1},... | collective-permute-start | bytes 835592 | tf_op jit(solution)/shard_map/ppermute | solution.py:401
  28.6 15.5 %collective-permute-start.5 = (bf16[64,2176]{1,0:T(8,128)(2,1)S(1)}, bf16[64,2176]{1,0:T(8,128)(2,1)S(1)}, u32[]{:S(2)}, u32[]{:S(2)}) collective-permute-start(bf16[64,2176]{1,0:T(8,128)(2,1)S(1)} %copy-done.8), channel_id=1, source_target_pairs={{0,4},{1,5},{2,6},{3,7},{4,8},{5,9},{6,10},{7,11},{8,12},{9,13},{1... | collective-permute-start | bytes 835592 | tf_op jit(solution)/shard_map/ppermute | solution.py:401
  34.4 9.7 %copy-start.9 = (bf16[64,2176]{1,0:T(8,128)(2,1)}, bf16[64,2176]{1,0:T(8,128)(2,1)S(1)}, u32[]{:S(2)}) copy-start(bf16[64,2176]{1,0:T(8,128)(2,1)S(1)} %collective-permute-done.7.refs_3_) | copy-start | bytes 835588
  34.4 15.6 %collective-permute-start.4 = (bf16[128,1024]{1,0:T(8,128)(2,1)S(1)}, bf16[128,1024]{1,0:T(8,128)(2,1)S(1)}, u32[]{:S(2)}, u32[]{:S(2)}) collective-permute-start(bf16[128,1024]{1,0:T(8,128)(2,1)S(1)} %constant_dynamic-update-slice_fusion.refs_0_), channel_id=1, source_target_pairs={{0,12},{1,13},{2,14},{3,15},{4,0},{5,1},{6,2},{7,3},{8,4},{9,5},{1... | collective-permute-start | bytes 786440 | tf_op jit(solution)/shard_map/ppermute | solution.py:401
  42.5 1.6 %copy-start.10 = (bf16[64,2176]{1,0:T(8,128)(2,1)}, bf16[64,2176]{1,0:T(8,128)(2,1)S(1)}, u32[]{:S(2)}) copy-start(bf16[64,2176]{1,0:T(8,128)(2,1)S(1)} %collective-permute-done.6.refs_2_) | copy-start | bytes 835588
  44.1 0.7 copy-start.11
  47.1 17.7 %collective-permute-start.8 = (bf16[256,1152]{1,0:T(8,128)(2,1)}, bf16[256,1152]{1,0:T(8,128)(2,1)S(1)}, u32[]{:S(2)}, u32[]{:S(2)}) collective-permute-start(bf16[256,1152]{1,0:T(8,128)(2,1)} %get-tuple-element.16.refs_0_.refs_2_), channel_id=1, source_target_pairs={{0,2},{1,3},{2,0},{3,1},{4,6},{5,7},{6,4},{7,5},{8,10},{9,11},{10,... | collective-permute-start | bytes 1769480 | tf_op jit(solution)/shard_map/ppermute | solution.py:393
  47.5 3.3 %copy-start.1 = (bf16[2,512,1024]{2,1,0:T(8,128)(2,1)S(1)}, bf16[2,512,1024]{2,1,0:T(8,128)(2,1)}, u32[]{:S(2)}) copy-start(bf16[2,512,1024]{2,1,0:T(8,128)(2,1)} %get-tuple-element.14.refs_0_.g0) | copy-start | bytes 6291460
  47.5 3.3 %copy-start.6 = (f32[64,64]{1,0:T(8,128)S(1)}, f32[64,64]{1,0:T(8,128)}, u32[]{:S(2)}) copy-start(f32[64,64]{1,0:T(8,128)} %table_ref.1) | copy-start | bytes 49156
  49.4 8.0 %collective-permute-start.3 = (bf16[128,1024]{1,0:T(8,128)(2,1)S(1)}, bf16[128,1024]{1,0:T(8,128)(2,1)S(1)}, u32[]{:S(2)}, u32[]{:S(2)}) collective-permute-start(bf16[128,1024]{1,0:T(8,128)(2,1)S(1)} %constant_dynamic-update-slice_fusion.refs_0_), channel_id=1, source_target_pairs={{0,8},{1,9},{2,10},{3,11},{4,12},{5,13},{6,14},{7,15},{8,0},{9,1},... | collective-permute-start | bytes 786440 | tf_op jit(solution)/shard_map/ppermute | solution.py:401
  50.1 0.7 copy-start.4
  50.8 14.1 %collective-permute-start.2 = (bf16[128,1024]{1,0:T(8,128)(2,1)S(1)}, bf16[128,1024]{1,0:T(8,128)(2,1)S(1)}, u32[]{:S(2)}, u32[]{:S(2)}) collective-permute-start(bf16[128,1024]{1,0:T(8,128)(2,1)S(1)} %constant_dynamic-update-slice_fusion.refs_0_), channel_id=1, source_target_pairs={{0,4},{1,5},{2,6},{3,7},{4,8},{5,9},{6,10},{7,11},{8,12},{9,13},{1... | collective-permute-start | bytes 786440 | tf_op jit(solution)/shard_map/ppermute | solution.py:401
  50.8 14.1 %copy-start.5 = (bf16[128,1024]{1,0:T(8,128)(2,1)S(1)}, bf16[128,1024]{1,0:T(8,128)(2,1)}, u32[]{:S(2)}) copy-start(bf16[128,1024]{1,0:T(8,128)(2,1)} %copy-done.4) | copy-start | bytes 786436
  51.6 16.2 %copy-start.17 = (s32[4]{0:T(128)S(1)}, s32[4]{0:T(128)}, u32[]{:S(2)}) copy-start(s32[4]{0:T(128)} %param.21) | copy-start | bytes 52
  51.6 16.4 %copy-start.16 = (s32[4096]{0:T(1024)S(1)}, s32[4096]{0:T(1024)}, u32[]{:S(2)}) copy-start(s32[4096]{0:T(1024)} %param.20) | copy-start | bytes 49156
  67.3 7.7 %collective-permute-start.9 = (bf16[1024,512]{1,0:T(8,128)(2,1)}, bf16[1024,512]{1,0:T(8,128)(2,1)}, u32[]{:S(2)}, u32[]{:S(2)}) collective-permute-start(bf16[1024,512]{1,0:T(8,128)(2,1)} %rotate_turned.1.t0), channel_id=1, source_target_pairs={{0,1},{1,0},{2,3},{3,2},{4,5},{5,4},{6,7},{7,6},{8,9},{9,8},{10,11... | collective-permute-start | bytes 3145736 | tf_op jit(solution)/shard_map/ppermute | solution.py:390
  68.0 2.8 %copy-start.3 = (bf16[256,1024]{1,0:T(8,128)(2,1)S(1)}, bf16[256,1024]{1,0:T(8,128)(2,1)}, u32[]{:S(2)}) copy-start(bf16[256,1024]{1,0:T(8,128)(2,1)} %get-tuple-element.17.refs_0_) | copy-start | bytes 1572868
  68.0 5.7 %copy-start = (bf16[256,1152]{1,0:T(8,128)(2,1)S(1)}, bf16[256,1152]{1,0:T(8,128)(2,1)}, u32[]{:S(2)}) copy-start(bf16[256,1152]{1,0:T(8,128)(2,1)} %get-tuple-element.16.refs_0_.refs_2_) | copy-start | bytes 1769476
  70.8 21.7 %collective-permute-start.10 = (bf16[256,1024]{1,0:T(8,128)(2,1)S(1)}, bf16[256,1024]{1,0:T(8,128)(2,1)S(1)}, u32[]{:S(2)}, u32[]{:S(2)}) collective-permute-start(bf16[256,1024]{1,0:T(8,128)(2,1)S(1)} %copy-done.3), channel_id=1, source_target_pairs={{0,2},{1,3},{2,0},{3,1},{4,6},{5,7},{6,4},{7,5},{8,10},{9,11},{10,... | collective-permute-start | bytes 1572872 | tf_op jit(solution)/shard_map/ppermute | solution.py:393
  73.7 1.6 %copy-start.7 = (bf16[2,512,1024]{2,1,0:T(8,128)(2,1)S(1)}, bf16[2,512,1024]{2,1,0:T(8,128)(2,1)}, u32[]{:S(2)}) copy-start(bf16[2,512,1024]{2,1,0:T(8,128)(2,1)} %get-tuple-element.18.a0) | copy-start | bytes 6291460
  111.3 1.0 copy-start.2
  113.9 1.2 collective-permute-start.13
  115.8 10.2 %all-to-all-start = ((f32[8,2,512]{2,1,0:T(2,128)}), f32[8,2,512]{2,1,0:T(2,128)S(1)}, u32[]{:S(2)}, u32[]{:S(2)}) async-start(f32[8,2,512]{2,1,0:T(2,128)} %broadcast_in_dim.23), calls=%async_computation | async-start | bytes 65536 | tf_op jit(solution)/shard_map/all_to_all | solution.py:458
  126.0 12.2 %copy-start.14 = (f32[2,512]{1,0:T(2,128)}, f32[2,512]{1,0:T(2,128)S(1)}, u32[]{:S(2)}) copy-start(f32[2,512]{1,0:T(2,128)S(1)} %reduce_sum.37) | copy-start | bytes 12292
  (1 other events, 0.7 us)

commit v2 on v1

--- a/solution.py
+++ b/solution.py
@@ -18,68 +18,54 @@
     return pltpu.CompilerParams(vmem_limit_bytes=mib * 2**20)
 
 
-def turned_train(train_out, train_in, out_basis, in_basis, core, after=()):
-    tokens = train_in.shape[0]
-    width = in_basis.shape[1]
-
-    def kernel(core_ref, out_ref, in_ref, outer_ref, inner_ref, *refs):
-        away_ref, own_ref, acts_ref = refs[-3:]
+def turned_pairs(tokens, basis, pick, groups, kept, core, after=()):
+    rows = tokens.shape[0]
+    width = basis.shape[1]
+
+    def kernel(core_ref, tokens_ref, basis_ref, *refs):
         step = pl.program_id(0)
-
-        @pl.when(step < 4)
-        def _():
-            turned = jnp.dot(out_ref[...], outer_ref[0], preferred_element_type=F32).astype(BF)
-
-            @pl.when(step < 2)
-            def _():
-                away_ref[0] = turned
-
-            @pl.when(step >= 2)
-            def _():
-                own_ref[0] = turned
-
-        @pl.when(step >= 4)
-        def _():
-            acts_ref[0] = jnp.dot(
-                in_ref[...], inner_ref[0], preferred_element_type=F32
-            ).astype(BF)
-
-    def outer(n, s):
-        n = jnp.minimum(n, 3)
-        return jnp.where(n < 2, (1 - s[0]) * 2 + n, s[0] * 2 + n - 2)
-
-    def inner(n, s):
-        return jnp.where(n < 5, s[0], 1 - s[0])
-
-    def result(first):
+        turned = jnp.dot(tokens_ref[...], basis_ref[0], preferred_element_type=F32).astype(BF)
+        for group in range(groups):
+
+            @pl.when(step // 2 == group)
+            def _(group=group):
+                refs[len(after) + group][0] = turned
+
+        for n, when in enumerate(kept):
+
+            @pl.when(step == when)
+            def _(n=n):
+                refs[len(after) + groups + n][...] = basis_ref[...]
+
+    def result(group):
         return pl.BlockSpec(
-            (1, tokens, width), lambda n, s: (jnp.clip(n - first, 0, 1), 0, 0)
+            (1, rows, width), lambda n, s: (jnp.clip(n - 2 * group, 0, 1), 0, 0)
         )
 
-    shape = jax.ShapeDtypeStruct((2, tokens, width), BF)
+    shape = jax.ShapeDtypeStruct((2, rows, width), BF)
     return pl.pallas_call(
         kernel,
         grid_spec=pltpu.PrefetchScalarGridSpec(
             num_scalar_prefetch=1,
-            grid=(6,),
+            grid=(2 * groups,),
             in_specs=[
-                pl.BlockSpec((tokens, width), lambda n, s: (0, outer(n, s))),
-                pl.BlockSpec((tokens, width), lambda n, s: (0, inner(n, s))),
-                pl.BlockSpec((1, width, width), lambda n, s: (outer(n, s), 0, 0)),
-                pl.BlockSpec((1, width, width), lambda n, s: (inner(n, s), 0, 0)),
+                pl.BlockSpec((rows, width), lambda n, s: (0, pick(n, s[0]))),
+                pl.BlockSpec((1, width, width), lambda n, s: (pick(n, s[0]), 0, 0)),
             ]
             + [UNREAD] * len(after),
-            out_specs=(result(0), result(2), result(4)),
-        ),
-        out_shape=(shape,) * 3,
+            out_specs=[result(group) for group in range(groups)]
+            + [pl.BlockSpec((1, width, width), lambda n, s: (0, 0, 0))] * len(kept),
+        ),
+        out_shape=[shape] * groups
+        + [jax.ShapeDtypeStruct((1, width, width), BF)] * len(kept),
         cost_estimate=pl.CostEstimate(
-            flops=12 * tokens * width * width,
-            bytes_accessed=12 * (2 * tokens * width + width * width),
+            flops=4 * groups * rows * width * width,
+            bytes_accessed=4 * groups * (2 * rows * width + width * width),
             transcendentals=0,
         ),
-        compiler_params=vmem_limit(60),
-        name="turned_train",
-    )(core[None], train_out, train_in, out_basis, in_basis, *after)
+        compiler_params=vmem_limit(50),
+        name="turned_pairs",
+    )(core[None], tokens, basis, *after)
 
 
 def level_picks(levels, ref):
@@ -128,7 +114,7 @@
         in_specs=[pl.BlockSpec((rows, columns), lambda n: (0, 0))] * count,
         out_specs=[pl.BlockSpec(shape, lambda n: (0, 0)) for shape in shapes],
         out_shape=[jax.ShapeDtypeStruct(shape, BF) for shape in shapes],
-        compiler_params=vmem_limit(60),
+        compiler_params=vmem_limit(8),
         name="gathered",
     )(*pieces)
 
@@ -207,7 +193,7 @@
         in_specs=[smem] + [pl.BlockSpec((few, total), lambda n: (0, 0))] * 2,
         out_specs=[pl.BlockSpec(shape, lambda n: (0, 0)) for shape in shapes],
         out_shape=[jax.ShapeDtypeStruct(shape, BF) for shape in shapes],
-        compiler_params=vmem_limit(60),
+        compiler_params=vmem_limit(8),
         name="pooled",
     )(core[None], kept, got)
 
@@ -239,7 +225,7 @@
             bytes_accessed=2 * (2 * count * rows * width + width * width),
             transcendentals=0,
         ),
-        compiler_params=vmem_limit(20),
+        compiler_params=vmem_limit(60),
         name="rotate_turned",
     )(which[None], *pieces, basis, *after)
 
@@ -397,10 +383,11 @@
         return lax.ppermute(a, ("col", "ex"), [(i, i ^ ex_count ^ 2) for i in range(count)])
 
     def along_x(a):
-        return [a] + [
-            lax.ppermute(a, "ex", [(i, (i + 4 * n) % ex_count) for i in range(ex_count)])
-            for n in range(1, hops)
-        ]
+        result = [a]
+        for n in range(1, hops):
+            pairs = [(i, (i + 4 * n) % ex_count) for i in range(ex_count)]
+            result.append(lax.ppermute(a, "ex", pairs))
+        return result
 
     kept, sent = parcels(query_in, query_out, query_ids, core)
     near_in, near_out = pooled(kept, to_core(sent), core, width)
@@ -408,12 +395,28 @@
     column = jnp.concatenate([near_in, near_in_y])
     row = along_x(near_out)
     rows = gathered(row, width + LANES)
-    grads_away, grads_own, acts_own = turned_train(
-        train_out, train_in, out_basis, in_basis, core, (near_in,)
+    grads_away, grads_own, *outers = turned_pairs(
+        train_out,
+        out_basis,
+        lambda n, c: jnp.where(n < 2, (1 - c) * 2 + n, c * 2 + n - 2),
+        2,
+        (2, 3),
+        core,
+        (near_in,),
     )
-    first_pieces, second_pieces = ([r, across_y(r)] for r in rows)
+    grads_other = to_core(grads_away)
     in_pieces = along_x(column)
-    grads_other = to_core(grads_away)
+    first_pieces = [rows[0], across_y(rows[0])]
+    second_pieces = [rows[1], across_y(rows[1])]
+    acts_own, inner = turned_pairs(
+        train_in,
+        in_basis,
+        lambda n, c: jnp.where(n < 1, c, 1 - c),
+        1,
+        (0,),
+        core,
+        (column, *rows),
+    )
     acts_other = to_core(acts_own)
 
     in_levels = in_level.reshape(in_sub, width)
@@ -421,11 +424,9 @@
         [lax.dynamic_slice_in_dim(in_levels, n, 1) for n in (core, 1 - core)], axis=1
     )
     out_levels = lax.dynamic_slice_in_dim(out_level, core * half * width, half * width)[None]
-    sides = inverse_sides(level_table, in_levels, (grads_own,))
-
-    inner = lax.dynamic_slice_in_dim(in_basis, core, 1)
-    outers = [lax.dynamic_slice_in_dim(out_basis, core * half + n, 1) for n in range(half)]
-    query_own = rotate_turned(in_pieces, inner, core, (sides, first_pieces[1]))
+    sides = inverse_sides(level_table, in_levels)
+
+    query_own = rotate_turned(in_pieces, inner, core)
     query_other = to_core(query_own)
     running = None
     for block, pieces in enumerate((first_pieces, second_pieces)):
@@ -448,21 +449,23 @@
             block,
         )
 
-    part = jnp.sum(running, axis=2)
-    mine, others = part[:, :tokens], part[:, tokens:]
-    token_part = mine + to_core(others)
-
     def sum_over(shard, axes):
         size = lax.axis_size(axes)
         spread = jnp.broadcast_to(shard[None], (size, *shard.shape))
         return jnp.sum(lax.all_to_all(spread, axes, 0, 0, tiled=True), axis=0)
 
-    token_scores = sum_over(token_part, ("row", "col"))
+    both = sum_over(jnp.sum(running, axis=2), ("row", "col"))
+    mine, others = both[:, :tokens], both[:, tokens:]
+    token_scores = mine + to_core(others)
     ends = jnp.cumsum(lengths)
     starts = ends - lengths
-    at = ex_index * tokens + jnp.arange(tokens, dtype=jnp.int32)
-    member = (at[None, :] >= starts[:, None]) & (at[None, :] < ends[:, None])
-    example_part = jnp.sum(jnp.where(member[None], token_scores[:, None, :], 0.0), axis=2)
+
+    def member(where):
+        at = where * tokens + jnp.arange(tokens, dtype=jnp.int32)
+        return (at[None, :] >= starts[:, None]) & (at[None, :] < ends[:, None])
+
+    members = jnp.concatenate([member(ex_index), member(ex_index ^ 1)], axis=1)
+    example_part = jnp.sum(jnp.where(members[None], both[:, None, :], 0.0), axis=2)
     example_scores = sum_over(example_part, "ex")
     return (token_scores, example_scores)
 

time: 139 us -> 137 us (0.986)
  local copies, waits for them, and re-layouts: 8.73 us -> 3.91 us
  waiting for transfers between devices: 27.2 us -> 29.6 us
  Pallas kernels: 60.8 us -> 62.8 us
    ppermute x2, waiting for transfers between devices: 0.01 us -> 11.3 us  [across_y(): return lax.ppermute(a, 'ex', [(i, i ^ 2) for i in range(ex_count)])]
    ppermute x6, waiting for transfers between devices: 20 us -> 11.9 us  [along_x(): result.append(lax.ppermute(a, 'ex', pairs))]
    dynamic_slice x2 -> x0, local copies, waits for them, and re-layouts: 4.67 us -> none  [the longest x1 2.76 us: body(): lax.dynamic_slice_in_dim(out_basis, core * half + n, 1)]
    ppermute x6, starting transfers between devices: 12.3 us -> 7.85 us  [along_x(): result.append(lax.ppermute(a, 'ex', pairs))]
    ppermute x5, starting transfers between devices: 2.99 us -> 7.4 us  [to_core(): return lax.ppermute(a, 'ex', [(i, i ^ 1) for i in range(ex_count)])]
    pallas_call x1 -> x2, Pallas kernels: 14.3 us -> 17.9 us  [turned_pairs(): pl.pallas_call(kernel, grid_spec=pltpu.PrefetchScalarGridSpec(num_scalar_...]
    pallas_call x1, Pallas kernels: 2.26 us -> 0.08 us  [gathered(): pl.pallas_call(kernel, grid=(1,), in_specs=[pl.BlockSpec((rows, columns),...]
    pallas_call x1, Pallas kernels: 2.44 us -> 4.42 us  [rotate_turned(): pl.pallas_call(kernel, grid_spec=pltpu.PrefetchScalarGridSpec(num_scalar_...]
  transfers between devices with their start and end apart: 15 -> 15, of which waited for: 7 -> 5; matrix products, arithmetic and copies ran while one was open for 4% -> 1% of each run, Pallas kernels for 28% -> 31%
where the time goes in v2:
time: 137 us
  Pallas kernels  62.8 us (46%)
  waiting for transfers between devices  29.6 us (22%)
  starting transfers between devices  26.3 us (19%)
  blocking collectives  11.7 us (9%)
  local copies, waits for them, and re-layouts  3.91 us (3%)
  other arithmetic  1.94 us (1%)
    pallas_call x2, Pallas kernels, score_block(): pl.pallas_call(kernel, grid=(strips,), in_specs=[turned_spec, turned_spec...  35.1 us
    pallas_call x2, Pallas kernels, turned_pairs(): pl.pallas_call(kernel, grid_spec=pltpu.PrefetchScalarGridSpec(num_scalar_...  17.9 us
    ppermute x6, waiting for transfers between devices, along_x(): result.append(lax.ppermute(a, 'ex', pairs))  11.9 us
    all_to_all x1, blocking collectives, sum_over(): return jnp.sum(lax.all_to_all(spread, axes, 0, 0, tiled=True), axis=0)  11.7 us
    ppermute x2, waiting for transfers between devices, across_y(): return lax.ppermute(a, 'ex', [(i, i ^ 2) for i in range(ex_count)])  11.3 us
    ppermute x6, starting transfers between devices, along_x(): result.append(lax.ppermute(a, 'ex', pairs))  7.85 us
    ppermute x5, starting transfers between devices, to_core(): return lax.ppermute(a, 'ex', [(i, i ^ 1) for i in range(ex_count)])  7.4 us
    all_to_all x1, waiting for transfers between devices, sum_over(): return jnp.sum(lax.all_to_all(spread, axes, 0, 0, tiled=True), axis=0)  5.18 us
  transfers between devices with their start and end apart: 15, of which 5 were waited for; matrix products, arithmetic and copies ran while one was open for 1% of the time, Pallas kernels for 31%

profile of v2, /device:TPU:1, one launch (start us, length us, event | category | flops | bytes accessed | tf_op | source)
XLA Modules:
  0.0 137.2 jit_solution(11593661974326132823)
XLA Ops:
  0.6 1.8 %parcels.1 = (bf16[32,3200]{1,0:T(8,128)(2,1)}, bf16[32,3200]{1,0:T(8,128)(2,1)}) custom-call(s32[1]{0:T(128)} %bitcast.core_ref.start_ref, s32[32]{0:T(128)} %ids_ref.1, bf16[32,2048]{1,0:T(8,128)(2,1)} %in_ref.1, bf16[32,4096]{1,0:T(8,128)(2,1)} %out_ref.1), custom_call_target="tpu_custom_call" | custom-call | tf_op jit(solution)/shard_map/parcels/pallas_call | solution.py:151
  2.5 1.4 %collective-permute-start = (bf16[32,3200]{1,0:T(8,128)(2,1)}, bf16[32,3200]{1,0:T(8,128)(2,1)S(1)}, u32[]{:S(2)}, u32[]{:S(2)}) collective-permute-start(bf16[32,3200]{1,0:T(8,128)(2,1)} %get-tuple-element.15), channel_id=1, source_target_pairs={{0,1},{1,0},{2,3},{3,2},{4,5},{5,4},{6,7},{7,6},{8,9},{9,8},{10,11... | collective-permute-start | bytes 614408 | tf_op jit(solution)/shard_map/ppermute | solution.py:376
  3.9 1.3 collective-permute-done.got_ref
  5.2 0.9 copy-done.8
  6.1 1.4 %collective-permute-start.5 = (bf16[64,2176]{1,0:T(8,128)(2,1)S(1)}, bf16[64,2176]{1,0:T(8,128)(2,1)S(1)}, u32[]{:S(2)}, u32[]{:S(2)}) collective-permute-start(bf16[64,2176]{1,0:T(8,128)(2,1)S(1)} %get-tuple-element.17.refs_0_), channel_id=1, source_target_pairs={{0,4},{1,5},{2,6},{3,7},{4,8},{5,9},{6,10},{7,11},{8,12},{9,13},{1... | collective-permute-start | bytes 835592 | tf_op jit(solution)/shard_map/ppermute | solution.py:389
  7.5 2.5 %collective-permute-start.6 = (bf16[64,2176]{1,0:T(8,128)(2,1)S(1)}, bf16[64,2176]{1,0:T(8,128)(2,1)S(1)}, u32[]{:S(2)}, u32[]{:S(2)}) collective-permute-start(bf16[64,2176]{1,0:T(8,128)(2,1)S(1)} %get-tuple-element.17.refs_0_), channel_id=1, source_target_pairs={{0,8},{1,9},{2,10},{3,11},{4,12},{5,13},{6,14},{7,15},{8,0},{9,1},... | collective-permute-start | bytes 835592 | tf_op jit(solution)/shard_map/ppermute | solution.py:389
  10.0 1.2 collective-permute-start.7
  11.1 2.7 %collective-permute-start.1 = (bf16[64,1024]{1,0:T(8,128)(2,1)S(1)}, bf16[64,1024]{1,0:T(8,128)(2,1)S(1)}, u32[]{:S(2)}, u32[]{:S(2)}) collective-permute-start(bf16[64,1024]{1,0:T(8,128)(2,1)S(1)} %get-tuple-element.16.refs_0_), channel_id=1, source_target_pairs={{0,18},{1,19},{2,16},{3,17},{4,22},{5,23},{6,20},{7,21},{8,26},{9,... | collective-permute-start | bytes 393224 | tf_op jit(solution)/shard_map/ppermute | solution.py:383
  13.9 11.3 %turned_pairs.3 = (bf16[2,512,1024]{2,1,0:T(8,128)(2,1)}, bf16[2,512,1024]{2,1,0:T(8,128)(2,1)}, bf16[1,1024,1024]{2,1,0:T(8,128)(2,1)}, bf16[1,1024,1024]{2,1,0:T(8,128)(2,1)}) custom-call(s32[1]{0:T(128)} %bitcast.core_ref.start_ref, bf16[512,4096]{1,0:T(8,128)(2,1)} %tokens_ref.3, bf16[4,1024,1024]{2,1,0:T(8,128)(2,1)} %basis_ref.3, ...), custom_call_target="tpu_custom_call" | custom-call | flops 4294967296 | bytes 16777216 | tf_op jit(solution)/shard_map/turned_pairs/pallas_call | solution.py:46
  25.1 1.6 %collective-permute-start.12 = (bf16[2,512,1024]{2,1,0:T(8,128)(2,1)}, bf16[2,512,1024]{2,1,0:T(8,128)(2,1)}, u32[]{:S(2)}, u32[]{:S(2)}) collective-permute-start(bf16[2,512,1024]{2,1,0:T(8,128)(2,1)} %get-tuple-element.25), channel_id=1, source_target_pairs={{0,1},{1,0},{2,3},{3,2},{4,5},{5,4},{6,7},{7,6},{8,9},{9,8},{10,11... | collective-permute-start | bytes 6291464 | tf_op jit(solution)/shard_map/ppermute | solution.py:376
  26.9 6.6 %turned_pairs.2 = (bf16[2,512,1024]{2,1,0:T(8,128)(2,1)}, bf16[1,1024,1024]{2,1,0:T(8,128)(2,1)}) custom-call(s32[1]{0:T(128)} %bitcast.core_ref.start_ref, bf16[512,2048]{1,0:T(8,128)(2,1)} %tokens_ref.2, bf16[2,1024,1024]{2,1,0:T(8,128)(2,1)} %basis_ref.2, bf16[128,1024]{1,0:T(8,128)(2,1)S(1)} %constant_dynamic-update-slice_fusion.refs_0_, ...), custom_call_target="tpu_custom_call" | custom-call | flops 2147483648 | bytes 8388608 | tf_op jit(solution)/shard_map/turned_pairs/pallas_call | solution.py:46
  34.0 0.6 collective-permute-start.3
  34.6 1.9 %collective-permute-start.4 = (bf16[128,1024]{1,0:T(8,128)(2,1)S(1)}, bf16[128,1024]{1,0:T(8,128)(2,1)S(1)}, u32[]{:S(2)}, u32[]{:S(2)}) collective-permute-start(bf16[128,1024]{1,0:T(8,128)(2,1)S(1)} %constant_dynamic-update-slice_fusion.refs_0_), channel_id=1, source_target_pairs={{0,12},{1,13},{2,14},{3,15},{4,0},{5,1},{6,2},{7,3},{8,4},{9,5},{1... | collective-permute-start | bytes 786440 | tf_op jit(solution)/shard_map/ppermute | solution.py:389
  36.5 11.5 %collective-permute-done.2.refs_1_ = bf16[128,1024]{1,0:T(8,128)(2,1)S(1)} collective-permute-done((bf16[128,1024]{1,0:T(8,128)(2,1)S(1)}, bf16[128,1024]{1,0:T(8,128)(2,1)S(1)}, u32[]{:S(2)}, u32[]{:S(2)}) %collective-permute-start.2) | collective-permute-done | bytes 262176 | tf_op jit(solution)/shard_map/ppermute | solution.py:389
  49.1 4.4 %rotate_turned.1.t0 = bf16[1024,512]{1,0:T(8,128)(2,1)} custom-call(s32[1]{0:T(128)} %bitcast.core_ref.start_ref, bf16[128,1024]{1,0:T(8,128)(2,1)} %copy-done.3, bf16[128,1024]{1,0:T(8,128)(2,1)} %copy-done.11, bf16[128,1024]{1,0:T(8,128)(2,1)} %copy-done.12, bf16[128,1024]{1,0:T(8,128)(2,1)} %copy-done.13, bf16[1,1024,1024]{2,1,0:T(8,128)(2,1)} %get-tuple-element.20.refs_4_), custom_call_target="tpu_custom_call" | custom-call | flops 1073741824 | bytes 4194304 | tf_op jit(solution)/shard_map/rotate_turned/pallas_call | solution.py:212
  53.5 1.5 %collective-permute-start.8 = (bf16[1024,512]{1,0:T(8,128)(2,1)}, bf16[1024,512]{1,0:T(8,128)(2,1)}, u32[]{:S(2)}, u32[]{:S(2)}) collective-permute-start(bf16[1024,512]{1,0:T(8,128)(2,1)} %rotate_turned.1.t0), channel_id=1, source_target_pairs={{0,1},{1,0},{2,3},{3,2},{4,5},{5,4},{6,7},{7,6},{8,9},{9,8},{10,11... | collective-permute-start | bytes 3145736 | tf_op jit(solution)/shard_map/ppermute | solution.py:376
  55.7 0.8 inverse_sides.1.sides_ref
  56.5 0.8 copy-done.6
  57.4 2.9 %collective-permute-start.9 = (bf16[256,1024]{1,0:T(8,128)(2,1)}, bf16[256,1024]{1,0:T(8,128)(2,1)S(1)}, u32[]{:S(2)}, u32[]{:S(2)}) collective-permute-start(bf16[256,1024]{1,0:T(8,128)(2,1)} %copy-done.4), channel_id=1, source_target_pairs={{0,2},{1,3},{2,0},{3,1},{4,6},{5,7},{6,4},{7,5},{8,10},{9,11},{10,... | collective-permute-start | bytes 1572872 | tf_op jit(solution)/shard_map/ppermute | solution.py:379
  60.3 11.3 %collective-permute-done.10.refs_1_.refs_3_ = bf16[256,1152]{1,0:T(8,128)(2,1)S(1)} collective-permute-done((bf16[256,1152]{1,0:T(8,128)(2,1)S(1)}, bf16[256,1152]{1,0:T(8,128)(2,1)S(1)}, u32[]{:S(2)}, u32[]{:S(2)}) %collective-permute-start.10) | collective-permute-done | bytes 589856 | tf_op jit(solution)/shard_map/ppermute | solution.py:379
  71.6 1.3 spread_out.2.spread_ref
  72.9 0.7 copy-done.10
  73.6 17.5 %score_block.2.refs_5_.refs_0_ = f32[2,1024,128]{2,1,0:T(8,128)S(1)} custom-call(bf16[1024,512]{1,0:T(8,128)(2,1)S(1)} %copy-done.2, bf16[1024,512]{1,0:T(8,128)(2,1)} %collective-permute-done.8.t1, bf16[2,512,1024]{2,1,0:T(8,128)(2,1)S(1)} %spread_out.2.spread_ref, bf16[2048,128]{1,0:T(8,128)(2,1)S(1)} %copy-done.7, s32[1,2048]{1,0:T(1,128)S(1)} %bitcast.5, ...), custom_call_target="tpu_custom_call" | custom-call | flops 12884901888 | bytes 16777216 | tf_op jit(solution)/shard_map/score_block/pallas_call | solution.py:325
  91.2 1.3 spread_out.3.spread_ref
  92.5 17.6 %score_block.3 = f32[2,1024,128]{2,1,0:T(8,128)S(1)} custom-call(bf16[1024,512]{1,0:T(8,128)(2,1)S(1)} %copy-done.2, bf16[1024,512]{1,0:T(8,128)(2,1)} %collective-permute-done.8.t1, bf16[2,512,1024]{2,1,0:T(8,128)(2,1)S(1)} %spread_out.3.spread_ref, bf16[2048,128]{1,0:T(8,128)(2,1)S(1)} %copy-done.7, s32[1,2048]{1,0:T(1,128)S(1)} %bitcast.6, ...), custom_call_target="tpu_custom_call" | custom-call | flops 12884901888 | bytes 16777216 | tf_op jit(solution)/shard_map/score_block/pallas_call | solution.py:325
  110.5 0.6 broadcast_in_dim.23
  111.1 5.0 %all-to-all-start = ((f32[8,2,1024]{2,1,0:T(2,128)}), f32[8,2,1024]{2,1,0:T(2,128)S(1)}, u32[]{:S(2)}, u32[]{:S(2)}) async-start(f32[8,2,1024]{2,1,0:T(2,128)} %broadcast_in_dim.23), calls=%async_computation | async-start | bytes 131072 | tf_op jit(solution)/shard_map/all_to_all | solution.py:455
  116.2 5.2 %all-to-all-done = f32[8,2,1024]{2,1,0:T(2,128)S(1)} async-done(((f32[8,2,1024]{2,1,0:T(2,128)}), f32[8,2,1024]{2,1,0:T(2,128)S(1)}, u32[]{:S(2)}, u32[]{:S(2)}) %all-to-all-start) | async-done | bytes 65568 | tf_op jit(solution)/shard_map/all_to_all | solution.py:455
  121.4 2.8 %collective-permute-start.13 = (f32[2,512]{1,0:T(2,128)S(1)}, f32[2,512]{1,0:T(2,128)S(1)}, u32[]{:S(2)}, u32[]{:S(2)}) collective-permute-start(f32[2,512]{1,0:T(2,128)S(1)} %slice.9), channel_id=1, source_target_pairs={{0,1},{1,0},{2,3},{3,2},{4,5},{5,4},{6,7},{7,6},{8,9},{9,8},{10,11... | collective-permute-start | bytes 12296 | tf_op jit(solution)/shard_map/ppermute | solution.py:376
  124.3 11.7 %all_to_all.10 = f32[16,2,4]{2,1,0:T(2,128)S(1)} all-to-all(f32[16,2,4]{2,1,0:T(2,128)S(1)} %broadcast_in_dim.27), channel_id=1, replica_groups=mesh['row'=4,'col'=2,'ex'=16] {'ex'}, dimensions={0} | all-to-all | bytes 1024 | tf_op jit(solution)/shard_map/all_to_all | solution.py:455
  136.0 0.6 reduce_sum.39
  136.6 0.6 slice_add_fusion
  (63 shorter events, 3.0 us)
Async XLA Ops:
  2.5 2.7 %collective-permute-start = (bf16[32,3200]{1,0:T(8,128)(2,1)}, bf16[32,3200]{1,0:T(8,128)(2,1)S(1)}, u32[]{:S(2)}, u32[]{:S(2)}) collective-permute-start(bf16[32,3200]{1,0:T(8,128)(2,1)} %get-tuple-element.15), channel_id=1, source_target_pairs={{0,1},{1,0},{2,3},{3,2},{4,5},{5,4},{6,7},{7,6},{8,9},{9,8},{10,11... | collective-permute-start | bytes 614408 | tf_op jit(solution)/shard_map/ppermute | solution.py:376
  5.2 0.9 copy-start.8
  6.1 20.6 %collective-permute-start.5 = (bf16[64,2176]{1,0:T(8,128)(2,1)S(1)}, bf16[64,2176]{1,0:T(8,128)(2,1)S(1)}, u32[]{:S(2)}, u32[]{:S(2)}) collective-permute-start(bf16[64,2176]{1,0:T(8,128)(2,1)S(1)} %get-tuple-element.17.refs_0_), channel_id=1, source_target_pairs={{0,4},{1,5},{2,6},{3,7},{4,8},{5,9},{6,10},{7,11},{8,12},{9,13},{1... | collective-permute-start | bytes 835592 | tf_op jit(solution)/shard_map/ppermute | solution.py:389
  7.5 19.3 %collective-permute-start.6 = (bf16[64,2176]{1,0:T(8,128)(2,1)S(1)}, bf16[64,2176]{1,0:T(8,128)(2,1)S(1)}, u32[]{:S(2)}, u32[]{:S(2)}) collective-permute-start(bf16[64,2176]{1,0:T(8,128)(2,1)S(1)} %get-tuple-element.17.refs_0_), channel_id=1, source_target_pairs={{0,8},{1,9},{2,10},{3,11},{4,12},{5,13},{6,14},{7,15},{8,0},{9,1},... | collective-permute-start | bytes 835592 | tf_op jit(solution)/shard_map/ppermute | solution.py:389
  10.0 16.8 %collective-permute-start.7 = (bf16[64,2176]{1,0:T(8,128)(2,1)S(1)}, bf16[64,2176]{1,0:T(8,128)(2,1)S(1)}, u32[]{:S(2)}, u32[]{:S(2)}) collective-permute-start(bf16[64,2176]{1,0:T(8,128)(2,1)S(1)} %get-tuple-element.17.refs_0_), channel_id=1, source_target_pairs={{0,12},{1,13},{2,14},{3,15},{4,0},{5,1},{6,2},{7,3},{8,4},{9,5},{1... | collective-permute-start | bytes 835592 | tf_op jit(solution)/shard_map/ppermute | solution.py:389
  11.1 15.6 %collective-permute-start.1 = (bf16[64,1024]{1,0:T(8,128)(2,1)S(1)}, bf16[64,1024]{1,0:T(8,128)(2,1)S(1)}, u32[]{:S(2)}, u32[]{:S(2)}) collective-permute-start(bf16[64,1024]{1,0:T(8,128)(2,1)S(1)} %get-tuple-element.16.refs_0_), channel_id=1, source_target_pairs={{0,18},{1,19},{2,16},{3,17},{4,22},{5,23},{6,20},{7,21},{8,26},{9,... | collective-permute-start | bytes 393224 | tf_op jit(solution)/shard_map/ppermute | solution.py:383
  25.1 47.7 %collective-permute-start.12 = (bf16[2,512,1024]{2,1,0:T(8,128)(2,1)}, bf16[2,512,1024]{2,1,0:T(8,128)(2,1)}, u32[]{:S(2)}, u32[]{:S(2)}) collective-permute-start(bf16[2,512,1024]{2,1,0:T(8,128)(2,1)} %get-tuple-element.25), channel_id=1, source_target_pairs={{0,1},{1,0},{2,3},{3,2},{4,5},{5,4},{6,7},{7,6},{8,9},{9,8},{10,11... | collective-permute-start | bytes 6291464 | tf_op jit(solution)/shard_map/ppermute | solution.py:376
  26.8 7.9 %copy-start.3 = (bf16[128,1024]{1,0:T(8,128)(2,1)}, bf16[128,1024]{1,0:T(8,128)(2,1)S(1)}, u32[]{:S(2)}) copy-start(bf16[128,1024]{1,0:T(8,128)(2,1)S(1)} %constant_dynamic-update-slice_fusion.refs_0_) | copy-start | bytes 786436
  26.9 6.7 %copy-start.4 = (bf16[256,1024]{1,0:T(8,128)(2,1)}, bf16[256,1024]{1,0:T(8,128)(2,1)S(1)}, u32[]{:S(2)}) copy-start(bf16[256,1024]{1,0:T(8,128)(2,1)S(1)} %get-tuple-element.19.refs_2_.refs_0_) | copy-start | bytes 1572868
  33.5 39.3 %collective-permute-start.11 = (bf16[2,512,1024]{2,1,0:T(8,128)(2,1)}, bf16[2,512,1024]{2,1,0:T(8,128)(2,1)}, u32[]{:S(2)}, u32[]{:S(2)}) collective-permute-start(bf16[2,512,1024]{2,1,0:T(8,128)(2,1)} %get-tuple-element.23.a0), channel_id=1, source_target_pairs={{0,1},{1,0},{2,3},{3,2},{4,5},{5,4},{6,7},{7,6},{8,9},{9,8},{10,11... | collective-permute-start | bytes 6291464 | tf_op jit(solution)/shard_map/ppermute | solution.py:376
  33.6 14.3 %collective-permute-start.2 = (bf16[128,1024]{1,0:T(8,128)(2,1)S(1)}, bf16[128,1024]{1,0:T(8,128)(2,1)S(1)}, u32[]{:S(2)}, u32[]{:S(2)}) collective-permute-start(bf16[128,1024]{1,0:T(8,128)(2,1)S(1)} %constant_dynamic-update-slice_fusion.refs_0_), channel_id=1, source_target_pairs={{0,4},{1,5},{2,6},{3,7},{4,8},{5,9},{6,10},{7,11},{8,12},{9,13},{1... | collective-permute-start | bytes 786440 | tf_op jit(solution)/shard_map/ppermute | solution.py:389
  34.0 14.0 %collective-permute-start.3 = (bf16[128,1024]{1,0:T(8,128)(2,1)S(1)}, bf16[128,1024]{1,0:T(8,128)(2,1)S(1)}, u32[]{:S(2)}, u32[]{:S(2)}) collective-permute-start(bf16[128,1024]{1,0:T(8,128)(2,1)S(1)} %constant_dynamic-update-slice_fusion.refs_0_), channel_id=1, source_target_pairs={{0,8},{1,9},{2,10},{3,11},{4,12},{5,13},{6,14},{7,15},{8,0},{9,1},... | collective-permute-start | bytes 786440 | tf_op jit(solution)/shard_map/ppermute | solution.py:389
  34.6 13.7 %collective-permute-start.4 = (bf16[128,1024]{1,0:T(8,128)(2,1)S(1)}, bf16[128,1024]{1,0:T(8,128)(2,1)S(1)}, u32[]{:S(2)}, u32[]{:S(2)}) collective-permute-start(bf16[128,1024]{1,0:T(8,128)(2,1)S(1)} %constant_dynamic-update-slice_fusion.refs_0_), channel_id=1, source_target_pairs={{0,12},{1,13},{2,14},{3,15},{4,0},{5,1},{6,2},{7,3},{8,4},{9,5},{1... | collective-permute-start | bytes 786440 | tf_op jit(solution)/shard_map/ppermute | solution.py:389
  48.0 0.7 copy-start.11
  48.0 0.8 copy-start.12
  48.4 0.7 copy-start.13
  49.1 6.0 %copy-start.14 = (s32[2048]{0:T(1024)S(1)}, s32[2048]{0:T(1024)}, u32[]{:S(2)}) copy-start(s32[2048]{0:T(1024)} %param.19) | copy-start | bytes 24580
  49.1 6.4 %copy-start.16 = (s32[4]{0:T(128)S(1)}, s32[4]{0:T(128)}, u32[]{:S(2)}) copy-start(s32[4]{0:T(128)} %param.21) | copy-start | bytes 52
  49.1 6.6 %copy-start.9 = (f32[64,64]{1,0:T(8,128)S(1)}, f32[64,64]{1,0:T(8,128)}, u32[]{:S(2)}) copy-start(f32[64,64]{1,0:T(8,128)} %table_ref.1) | copy-start | bytes 49156
  49.1 8.2 %copy-start.15 = (s32[4096]{0:T(1024)S(1)}, s32[4096]{0:T(1024)}, u32[]{:S(2)}) copy-start(s32[4096]{0:T(1024)} %param.20) | copy-start | bytes 49156
  49.1 22.5 %copy-start = (bf16[1,1024,1024]{2,1,0:T(8,128)(2,1)S(1)}, bf16[1,1024,1024]{2,1,0:T(8,128)(2,1)}, u32[]{:S(2)}) copy-start(bf16[1,1024,1024]{2,1,0:T(8,128)(2,1)} %get-tuple-element.22.refs_2_) | copy-start | bytes 6291460
  53.5 19.4 %collective-permute-start.8 = (bf16[1024,512]{1,0:T(8,128)(2,1)}, bf16[1024,512]{1,0:T(8,128)(2,1)}, u32[]{:S(2)}, u32[]{:S(2)}) collective-permute-start(bf16[1024,512]{1,0:T(8,128)(2,1)} %rotate_turned.1.t0), channel_id=1, source_target_pairs={{0,1},{1,0},{2,3},{3,2},{4,5},{5,4},{6,7},{7,6},{8,9},{9,8},{10,11... | collective-permute-start | bytes 3145736 | tf_op jit(solution)/shard_map/ppermute | solution.py:376
  55.1 16.5 %collective-permute-start.10 = (bf16[256,1152]{1,0:T(8,128)(2,1)S(1)}, bf16[256,1152]{1,0:T(8,128)(2,1)S(1)}, u32[]{:S(2)}, u32[]{:S(2)}) collective-permute-start(bf16[256,1152]{1,0:T(8,128)(2,1)S(1)} %get-tuple-element.18.refs_1_.refs_0_.refs_2_), channel_id=1, source_target_pairs={{0,2},{1,3},{2,0},{3,1},{4,6},{5,7},{6,4},{7,5},{8,10},{9,11},{10,... | collective-permute-start | bytes 1769480 | tf_op jit(solution)/shard_map/ppermute | solution.py:379
  56.5 0.8 copy-start.6
  57.4 33.7 %collective-permute-start.9 = (bf16[256,1024]{1,0:T(8,128)(2,1)}, bf16[256,1024]{1,0:T(8,128)(2,1)S(1)}, u32[]{:S(2)}, u32[]{:S(2)}) collective-permute-start(bf16[256,1024]{1,0:T(8,128)(2,1)} %copy-done.4), channel_id=1, source_target_pairs={{0,2},{1,3},{2,0},{3,1},{4,6},{5,7},{6,4},{7,5},{8,10},{9,11},{10,... | collective-permute-start | bytes 1572872 | tf_op jit(solution)/shard_map/ppermute | solution.py:379
  71.5 1.4 copy-start.2
  71.5 1.4 copy-start.7
  71.5 2.1 %copy-start.10 = (bf16[2,512,1024]{2,1,0:T(8,128)(2,1)S(1)}, bf16[2,512,1024]{2,1,0:T(8,128)(2,1)}, u32[]{:S(2)}) copy-start(bf16[2,512,1024]{2,1,0:T(8,128)(2,1)} %get-tuple-element.24.g0) | copy-start | bytes 6291460
  73.6 17.5 %copy-start.1 = (bf16[1,1024,1024]{2,1,0:T(8,128)(2,1)S(1)}, bf16[1,1024,1024]{2,1,0:T(8,128)(2,1)}, u32[]{:S(2)}) copy-start(bf16[1,1024,1024]{2,1,0:T(8,128)(2,1)} %get-tuple-element.21.refs_4_) | copy-start | bytes 6291460
  73.6 17.5 %copy-start.5 = (bf16[256,1024]{1,0:T(8,128)(2,1)S(1)}, bf16[256,1024]{1,0:T(8,128)(2,1)}, u32[]{:S(2)}) copy-start(bf16[256,1024]{1,0:T(8,128)(2,1)} %copy-done.4) | copy-start | bytes 1572868
  111.1 10.2 %all-to-all-start = ((f32[8,2,1024]{2,1,0:T(2,128)}), f32[8,2,1024]{2,1,0:T(2,128)S(1)}, u32[]{:S(2)}, u32[]{:S(2)}) async-start(f32[8,2,1024]{2,1,0:T(2,128)} %broadcast_in_dim.23), calls=%async_computation | async-start | bytes 131072 | tf_op jit(solution)/shard_map/all_to_all | solution.py:455
  121.4 15.2 %collective-permute-start.13 = (f32[2,512]{1,0:T(2,128)S(1)}, f32[2,512]{1,0:T(2,128)S(1)}, u32[]{:S(2)}, u32[]{:S(2)}) collective-permute-start(f32[2,512]{1,0:T(2,128)S(1)} %slice.9), channel_id=1, source_target_pairs={{0,1},{1,0},{2,3},{3,2},{4,5},{5,4},{6,7},{7,6},{8,9},{9,8},{10,11... | collective-permute-start | bytes 12296 | tf_op jit(solution)/shard_map/ppermute | solution.py:376

commit v3 on v2

--- a/solution.py
+++ b/solution.py
@@ -280,11 +280,17 @@
 
     levels = sides.shape[1] // 2
 
-    def kernel(t0, t1, spread_ref, sides_ref, levels_ref, a0, a1, g0, g1, *refs):
-        out_ref, scratch, inverse_ref = refs[-3:]
+    def kernel(t0, t1, spread_ref, sides_ref, levels_ref, far0, far1, g0, g1, *refs):
+        out_ref, scratch, inverse_ref, a0, a1, semaphores = refs[-6:]
+        copies = [
+            pltpu.make_async_copy(far, near, semaphores.at[n])
+            for n, (far, near) in enumerate(((far0, a0), (far1, a1)))
+        ]
 
         @pl.when(pl.program_id(0) == 0)
         def _():
+            for copy in copies:
+                copy.start()
             out_ref[...] = jnp.zeros(total_shape, F32) if running is None else refs[0][...]
 
         chosen = level_picks(levels, levels_ref)
@@ -299,6 +305,13 @@
                     at = slice(p * width + top, p * width + top + rows)
                     piece = jnp.dot(t[top : top + rows], spread_ref[q], preferred_element_type=F32)
                     scratch[at] = (piece * inverse_ref[at]).astype(BF)
+            if q == 0:
+
+                @pl.when(pl.program_id(0) == 0)
+                def _():
+                    for copy in copies:
+                        copy.wait()
+
             for side, (a, g) in enumerate(((a0, g0), (a1, g1))):
                 for top in range(0, tokens, rows):
                     image = None
@@ -317,7 +330,7 @@
                     out_ref[q, at : at + rows] += total
 
     once = pl.Buffered(1)
-    whole = pl.BlockSpec(acts[0].shape, lambda n: (0, 0, 0), pipeline_mode=once)
+    whole = pl.BlockSpec(memory_space=pltpu.HBM)
     turned_spec = pl.BlockSpec((width, qtokens), lambda n: (0, 0), pipeline_mode=once)
     strip_spec = pl.BlockSpec((1, tokens, strip), lambda n: (block, 0, n))
     run_spec = pl.BlockSpec(total_shape, lambda n: (0, 0, 0), pipeline_mode=once)
@@ -342,6 +355,9 @@
         scratch_shapes=[
             pltpu.VMEM((parts * width, strip), BF),
             pltpu.VMEM((parts * width, strip), F32),
+            pltpu.VMEM(acts[0].shape, BF),
+            pltpu.VMEM(acts[0].shape, BF),
+            pltpu.SemaphoreType.DMA((2,)),
         ],
         cost_estimate=pl.CostEstimate(flops=flops, bytes_accessed=16 * 2**20, transcendentals=0),
         compiler_params=vmem_limit(32),

time: 137 us -> 136 us (level)
  transfers between devices with their start and end apart: 15 -> 15, of which waited for: 5 -> 5; matrix products, arithmetic and copies ran while one was open for 1% -> 1% of each run, Pallas kernels for 31% -> 30%
where the time goes in v3:
time: 136 us
  Pallas kernels  61.7 us (45%)
  waiting for transfers between devices  29.6 us (22%)
  starting transfers between devices  26.3 us (19%)
  blocking collectives  11.7 us (9%)
  local copies, waits for them, and re-layouts  3.91 us (3%)
  other arithmetic  1.94 us (1%)
    pallas_call x2, Pallas kernels, score_block(): pl.pallas_call(kernel, grid=(strips,), in_specs=[turned_spec, turned_spec...  33.9 us
    pallas_call x2, Pallas kernels, turned_pairs(): pl.pallas_call(kernel, grid_spec=pltpu.PrefetchScalarGridSpec(num_scalar_...  17.9 us
    ppermute x6, waiting for transfers between devices, along_x(): result.append(lax.ppermute(a, 'ex', pairs))  11.9 us
    all_to_all x1, blocking collectives, sum_over(): return jnp.sum(lax.all_to_all(spread, axes, 0, 0, tiled=True), axis=0)  11.7 us
    ppermute x2, waiting for transfers between devices, across_y(): return lax.ppermute(a, 'ex', [(i, i ^ 2) for i in range(ex_count)])  11.3 us
    ppermute x6, starting transfers between devices, along_x(): result.append(lax.ppermute(a, 'ex', pairs))  7.85 us
    ppermute x5, starting transfers between devices, to_core(): return lax.ppermute(a, 'ex', [(i, i ^ 1) for i in range(ex_count)])  7.4 us
    all_to_all x1, waiting for transfers between devices, sum_over(): return jnp.sum(lax.all_to_all(spread, axes, 0, 0, tiled=True), axis=0)  5.18 us
  transfers between devices with their start and end apart: 15, of which 5 were waited for; matrix products, arithmetic and copies ran while one was open for 1% of the time, Pallas kernels for 30%

profile of v3, /device:TPU:1, one launch (start us, length us, event | category | flops | bytes accessed | tf_op | source)
XLA Modules:
  0.0 136.0 jit_solution(3438475024506295297)
XLA Ops:
  0.6 1.8 %parcels.1 = (bf16[32,3200]{1,0:T(8,128)(2,1)}, bf16[32,3200]{1,0:T(8,128)(2,1)}) custom-call(s32[1]{0:T(128)} %bitcast.core_ref.start_ref, s32[32]{0:T(128)} %ids_ref.1, bf16[32,2048]{1,0:T(8,128)(2,1)} %in_ref.1, bf16[32,4096]{1,0:T(8,128)(2,1)} %out_ref.1), custom_call_target="tpu_custom_call" | custom-call | tf_op jit(solution)/shard_map/parcels/pallas_call | solution.py:151
  2.5 1.4 %collective-permute-start = (bf16[32,3200]{1,0:T(8,128)(2,1)}, bf16[32,3200]{1,0:T(8,128)(2,1)S(1)}, u32[]{:S(2)}, u32[]{:S(2)}) collective-permute-start(bf16[32,3200]{1,0:T(8,128)(2,1)} %get-tuple-element.15), channel_id=1, source_target_pairs={{0,1},{1,0},{2,3},{3,2},{4,5},{5,4},{6,7},{7,6},{8,9},{9,8},{10,11... | collective-permute-start | bytes 614408 | tf_op jit(solution)/shard_map/ppermute | solution.py:392
  3.9 1.3 collective-permute-done.got_ref
  5.2 0.9 copy-done.8
  6.1 1.4 %collective-permute-start.5 = (bf16[64,2176]{1,0:T(8,128)(2,1)S(1)}, bf16[64,2176]{1,0:T(8,128)(2,1)S(1)}, u32[]{:S(2)}, u32[]{:S(2)}) collective-permute-start(bf16[64,2176]{1,0:T(8,128)(2,1)S(1)} %get-tuple-element.17.refs_0_), channel_id=1, source_target_pairs={{0,4},{1,5},{2,6},{3,7},{4,8},{5,9},{6,10},{7,11},{8,12},{9,13},{1... | collective-permute-start | bytes 835592 | tf_op jit(solution)/shard_map/ppermute | solution.py:405
  7.5 2.5 %collective-permute-start.6 = (bf16[64,2176]{1,0:T(8,128)(2,1)S(1)}, bf16[64,2176]{1,0:T(8,128)(2,1)S(1)}, u32[]{:S(2)}, u32[]{:S(2)}) collective-permute-start(bf16[64,2176]{1,0:T(8,128)(2,1)S(1)} %get-tuple-element.17.refs_0_), channel_id=1, source_target_pairs={{0,8},{1,9},{2,10},{3,11},{4,12},{5,13},{6,14},{7,15},{8,0},{9,1},... | collective-permute-start | bytes 835592 | tf_op jit(solution)/shard_map/ppermute | solution.py:405
  10.0 1.2 collective-permute-start.7
  11.1 2.7 %collective-permute-start.1 = (bf16[64,1024]{1,0:T(8,128)(2,1)S(1)}, bf16[64,1024]{1,0:T(8,128)(2,1)S(1)}, u32[]{:S(2)}, u32[]{:S(2)}) collective-permute-start(bf16[64,1024]{1,0:T(8,128)(2,1)S(1)} %get-tuple-element.16.refs_0_), channel_id=1, source_target_pairs={{0,18},{1,19},{2,16},{3,17},{4,22},{5,23},{6,20},{7,21},{8,26},{9,... | collective-permute-start | bytes 393224 | tf_op jit(solution)/shard_map/ppermute | solution.py:399
  13.9 11.3 %turned_pairs.3 = (bf16[2,512,1024]{2,1,0:T(8,128)(2,1)}, bf16[2,512,1024]{2,1,0:T(8,128)(2,1)}, bf16[1,1024,1024]{2,1,0:T(8,128)(2,1)}, bf16[1,1024,1024]{2,1,0:T(8,128)(2,1)}) custom-call(s32[1]{0:T(128)} %bitcast.core_ref.start_ref, bf16[512,4096]{1,0:T(8,128)(2,1)} %tokens_ref.3, bf16[4,1024,1024]{2,1,0:T(8,128)(2,1)} %basis_ref.3, ...), custom_call_target="tpu_custom_call" | custom-call | flops 4294967296 | bytes 16777216 | tf_op jit(solution)/shard_map/turned_pairs/pallas_call | solution.py:46
  25.1 1.6 %collective-permute-start.12 = (bf16[2,512,1024]{2,1,0:T(8,128)(2,1)}, bf16[2,512,1024]{2,1,0:T(8,128)(2,1)}, u32[]{:S(2)}, u32[]{:S(2)}) collective-permute-start(bf16[2,512,1024]{2,1,0:T(8,128)(2,1)} %get-tuple-element.25), channel_id=1, source_target_pairs={{0,1},{1,0},{2,3},{3,2},{4,5},{5,4},{6,7},{7,6},{8,9},{9,8},{10,11... | collective-permute-start | bytes 6291464 | tf_op jit(solution)/shard_map/ppermute | solution.py:392
  26.9 6.6 %turned_pairs.2 = (bf16[2,512,1024]{2,1,0:T(8,128)(2,1)}, bf16[1,1024,1024]{2,1,0:T(8,128)(2,1)}) custom-call(s32[1]{0:T(128)} %bitcast.core_ref.start_ref, bf16[512,2048]{1,0:T(8,128)(2,1)} %tokens_ref.2, bf16[2,1024,1024]{2,1,0:T(8,128)(2,1)} %basis_ref.2, bf16[128,1024]{1,0:T(8,128)(2,1)S(1)} %constant_dynamic-update-slice_fusion.refs_0_, ...), custom_call_target="tpu_custom_call" | custom-call | flops 2147483648 | bytes 8388608 | tf_op jit(solution)/shard_map/turned_pairs/pallas_call | solution.py:46
  34.0 0.6 collective-permute-start.3
  34.6 1.9 %collective-permute-start.4 = (bf16[128,1024]{1,0:T(8,128)(2,1)S(1)}, bf16[128,1024]{1,0:T(8,128)(2,1)S(1)}, u32[]{:S(2)}, u32[]{:S(2)}) collective-permute-start(bf16[128,1024]{1,0:T(8,128)(2,1)S(1)} %constant_dynamic-update-slice_fusion.refs_0_), channel_id=1, source_target_pairs={{0,12},{1,13},{2,14},{3,15},{4,0},{5,1},{6,2},{7,3},{8,4},{9,5},{1... | collective-permute-start | bytes 786440 | tf_op jit(solution)/shard_map/ppermute | solution.py:405
  36.5 11.5 %collective-permute-done.2.refs_1_ = bf16[128,1024]{1,0:T(8,128)(2,1)S(1)} collective-permute-done((bf16[128,1024]{1,0:T(8,128)(2,1)S(1)}, bf16[128,1024]{1,0:T(8,128)(2,1)S(1)}, u32[]{:S(2)}, u32[]{:S(2)}) %collective-permute-start.2) | collective-permute-done | bytes 262176 | tf_op jit(solution)/shard_map/ppermute | solution.py:405
  49.1 4.4 %rotate_turned.1.t0 = bf16[1024,512]{1,0:T(8,128)(2,1)} custom-call(s32[1]{0:T(128)} %bitcast.core_ref.start_ref, bf16[128,1024]{1,0:T(8,128)(2,1)} %copy-done.3, bf16[128,1024]{1,0:T(8,128)(2,1)} %copy-done.11, bf16[128,1024]{1,0:T(8,128)(2,1)} %copy-done.12, bf16[128,1024]{1,0:T(8,128)(2,1)} %copy-done.13, bf16[1,1024,1024]{2,1,0:T(8,128)(2,1)} %get-tuple-element.20.refs_4_), custom_call_target="tpu_custom_call" | custom-call | flops 1073741824 | bytes 4194304 | tf_op jit(solution)/shard_map/rotate_turned/pallas_call | solution.py:212
  53.5 1.5 %collective-permute-start.8 = (bf16[1024,512]{1,0:T(8,128)(2,1)}, bf16[1024,512]{1,0:T(8,128)(2,1)}, u32[]{:S(2)}, u32[]{:S(2)}) collective-permute-start(bf16[1024,512]{1,0:T(8,128)(2,1)} %rotate_turned.1.t0), channel_id=1, source_target_pairs={{0,1},{1,0},{2,3},{3,2},{4,5},{5,4},{6,7},{7,6},{8,9},{9,8},{10,11... | collective-permute-start | bytes 3145736 | tf_op jit(solution)/shard_map/ppermute | solution.py:392
  55.7 0.8 inverse_sides.1.sides_ref
  56.5 0.8 copy-done.6
  57.4 2.9 %collective-permute-start.9 = (bf16[256,1024]{1,0:T(8,128)(2,1)}, bf16[256,1024]{1,0:T(8,128)(2,1)S(1)}, u32[]{:S(2)}, u32[]{:S(2)}) collective-permute-start(bf16[256,1024]{1,0:T(8,128)(2,1)} %copy-done.4), channel_id=1, source_target_pairs={{0,2},{1,3},{2,0},{3,1},{4,6},{5,7},{6,4},{7,5},{8,10},{9,11},{10,... | collective-permute-start | bytes 1572872 | tf_op jit(solution)/shard_map/ppermute | solution.py:395
  60.3 11.3 %collective-permute-done.10.refs_1_.refs_3_ = bf16[256,1152]{1,0:T(8,128)(2,1)S(1)} collective-permute-done((bf16[256,1152]{1,0:T(8,128)(2,1)S(1)}, bf16[256,1152]{1,0:T(8,128)(2,1)S(1)}, u32[]{:S(2)}, u32[]{:S(2)}) %collective-permute-start.10) | collective-permute-done | bytes 589856 | tf_op jit(solution)/shard_map/ppermute | solution.py:395
  71.6 1.3 spread_out.2.spread_ref
  72.9 0.7 copy-done.10
  73.6 16.9 %score_block.2.refs_5_.refs_0_ = f32[2,1024,128]{2,1,0:T(8,128)S(1)} custom-call(bf16[1024,512]{1,0:T(8,128)(2,1)S(1)} %copy-done.2, bf16[1024,512]{1,0:T(8,128)(2,1)} %collective-permute-done.8.t1, bf16[2,512,1024]{2,1,0:T(8,128)(2,1)S(1)} %spread_out.2.spread_ref, bf16[2048,128]{1,0:T(8,128)(2,1)S(1)} %copy-done.7, s32[1,2048]{1,0:T(1,128)S(1)} %bitcast.5, ...), custom_call_target="tpu_custom_call" | custom-call | flops 12884901888 | bytes 16777216 | tf_op jit(solution)/shard_map/score_block/pallas_call | solution.py:338
  90.6 1.3 spread_out.3.spread_ref
  91.9 17.0 %score_block.3 = f32[2,1024,128]{2,1,0:T(8,128)S(1)} custom-call(bf16[1024,512]{1,0:T(8,128)(2,1)S(1)} %copy-done.2, bf16[1024,512]{1,0:T(8,128)(2,1)} %collective-permute-done.8.t1, bf16[2,512,1024]{2,1,0:T(8,128)(2,1)S(1)} %spread_out.3.spread_ref, bf16[2048,128]{1,0:T(8,128)(2,1)S(1)} %copy-done.7, s32[1,2048]{1,0:T(1,128)S(1)} %bitcast.6, ...), custom_call_target="tpu_custom_call" | custom-call | flops 12884901888 | bytes 16777216 | tf_op jit(solution)/shard_map/score_block/pallas_call | solution.py:338
  109.3 0.6 broadcast_in_dim.23
  109.9 5.0 %all-to-all-start = ((f32[8,2,1024]{2,1,0:T(2,128)}), f32[8,2,1024]{2,1,0:T(2,128)S(1)}, u32[]{:S(2)}, u32[]{:S(2)}) async-start(f32[8,2,1024]{2,1,0:T(2,128)} %broadcast_in_dim.23), calls=%async_computation | async-start | bytes 131072 | tf_op jit(solution)/shard_map/all_to_all | solution.py:471
  115.0 5.2 %all-to-all-done = f32[8,2,1024]{2,1,0:T(2,128)S(1)} async-done(((f32[8,2,1024]{2,1,0:T(2,128)}), f32[8,2,1024]{2,1,0:T(2,128)S(1)}, u32[]{:S(2)}, u32[]{:S(2)}) %all-to-all-start) | async-done | bytes 65568 | tf_op jit(solution)/shard_map/all_to_all | solution.py:471
  120.2 2.8 %collective-permute-start.13 = (f32[2,512]{1,0:T(2,128)S(1)}, f32[2,512]{1,0:T(2,128)S(1)}, u32[]{:S(2)}, u32[]{:S(2)}) collective-permute-start(f32[2,512]{1,0:T(2,128)S(1)} %slice.9), channel_id=1, source_target_pairs={{0,1},{1,0},{2,3},{3,2},{4,5},{5,4},{6,7},{7,6},{8,9},{9,8},{10,11... | collective-permute-start | bytes 12296 | tf_op jit(solution)/shard_map/ppermute | solution.py:392
  123.2 11.7 %all_to_all.10 = f32[16,2,4]{2,1,0:T(2,128)S(1)} all-to-all(f32[16,2,4]{2,1,0:T(2,128)S(1)} %broadcast_in_dim.27), channel_id=1, replica_groups=mesh['row'=4,'col'=2,'ex'=16] {'ex'}, dimensions={0} | all-to-all | bytes 1024 | tf_op jit(solution)/shard_map/all_to_all | solution.py:471
  134.8 0.6 reduce_sum.39
  135.4 0.6 slice_add_fusion
  (63 shorter events, 3.0 us)
Async XLA Ops:
  2.5 2.7 %collective-permute-start = (bf16[32,3200]{1,0:T(8,128)(2,1)}, bf16[32,3200]{1,0:T(8,128)(2,1)S(1)}, u32[]{:S(2)}, u32[]{:S(2)}) collective-permute-start(bf16[32,3200]{1,0:T(8,128)(2,1)} %get-tuple-element.15), channel_id=1, source_target_pairs={{0,1},{1,0},{2,3},{3,2},{4,5},{5,4},{6,7},{7,6},{8,9},{9,8},{10,11... | collective-permute-start | bytes 614408 | tf_op jit(solution)/shard_map/ppermute | solution.py:392
  5.2 0.9 copy-start.8
  6.1 20.6 %collective-permute-start.5 = (bf16[64,2176]{1,0:T(8,128)(2,1)S(1)}, bf16[64,2176]{1,0:T(8,128)(2,1)S(1)}, u32[]{:S(2)}, u32[]{:S(2)}) collective-permute-start(bf16[64,2176]{1,0:T(8,128)(2,1)S(1)} %get-tuple-element.17.refs_0_), channel_id=1, source_target_pairs={{0,4},{1,5},{2,6},{3,7},{4,8},{5,9},{6,10},{7,11},{8,12},{9,13},{1... | collective-permute-start | bytes 835592 | tf_op jit(solution)/shard_map/ppermute | solution.py:405
  7.5 19.3 %collective-permute-start.6 = (bf16[64,2176]{1,0:T(8,128)(2,1)S(1)}, bf16[64,2176]{1,0:T(8,128)(2,1)S(1)}, u32[]{:S(2)}, u32[]{:S(2)}) collective-permute-start(bf16[64,2176]{1,0:T(8,128)(2,1)S(1)} %get-tuple-element.17.refs_0_), channel_id=1, source_target_pairs={{0,8},{1,9},{2,10},{3,11},{4,12},{5,13},{6,14},{7,15},{8,0},{9,1},... | collective-permute-start | bytes 835592 | tf_op jit(solution)/shard_map/ppermute | solution.py:405
  10.0 16.8 %collective-permute-start.7 = (bf16[64,2176]{1,0:T(8,128)(2,1)S(1)}, bf16[64,2176]{1,0:T(8,128)(2,1)S(1)}, u32[]{:S(2)}, u32[]{:S(2)}) collective-permute-start(bf16[64,2176]{1,0:T(8,128)(2,1)S(1)} %get-tuple-element.17.refs_0_), channel_id=1, source_target_pairs={{0,12},{1,13},{2,14},{3,15},{4,0},{5,1},{6,2},{7,3},{8,4},{9,5},{1... | collective-permute-start | bytes 835592 | tf_op jit(solution)/shard_map/ppermute | solution.py:405
  11.1 15.6 %collective-permute-start.1 = (bf16[64,1024]{1,0:T(8,128)(2,1)S(1)}, bf16[64,1024]{1,0:T(8,128)(2,1)S(1)}, u32[]{:S(2)}, u32[]{:S(2)}) collective-permute-start(bf16[64,1024]{1,0:T(8,128)(2,1)S(1)} %get-tuple-element.16.refs_0_), channel_id=1, source_target_pairs={{0,18},{1,19},{2,16},{3,17},{4,22},{5,23},{6,20},{7,21},{8,26},{9,... | collective-permute-start | bytes 393224 | tf_op jit(solution)/shard_map/ppermute | solution.py:399
  25.1 47.7 %collective-permute-start.12 = (bf16[2,512,1024]{2,1,0:T(8,128)(2,1)}, bf16[2,512,1024]{2,1,0:T(8,128)(2,1)}, u32[]{:S(2)}, u32[]{:S(2)}) collective-permute-start(bf16[2,512,1024]{2,1,0:T(8,128)(2,1)} %get-tuple-element.25), channel_id=1, source_target_pairs={{0,1},{1,0},{2,3},{3,2},{4,5},{5,4},{6,7},{7,6},{8,9},{9,8},{10,11... | collective-permute-start | bytes 6291464 | tf_op jit(solution)/shard_map/ppermute | solution.py:392
  26.8 7.9 %copy-start.3 = (bf16[128,1024]{1,0:T(8,128)(2,1)}, bf16[128,1024]{1,0:T(8,128)(2,1)S(1)}, u32[]{:S(2)}) copy-start(bf16[128,1024]{1,0:T(8,128)(2,1)S(1)} %constant_dynamic-update-slice_fusion.refs_0_) | copy-start | bytes 786436
  26.9 6.7 %copy-start.4 = (bf16[256,1024]{1,0:T(8,128)(2,1)}, bf16[256,1024]{1,0:T(8,128)(2,1)S(1)}, u32[]{:S(2)}) copy-start(bf16[256,1024]{1,0:T(8,128)(2,1)S(1)} %get-tuple-element.19.refs_2_.refs_0_) | copy-start | bytes 1572868
  33.5 39.3 %collective-permute-start.11 = (bf16[2,512,1024]{2,1,0:T(8,128)(2,1)}, bf16[2,512,1024]{2,1,0:T(8,128)(2,1)}, u32[]{:S(2)}, u32[]{:S(2)}) collective-permute-start(bf16[2,512,1024]{2,1,0:T(8,128)(2,1)} %get-tuple-element.23.far0), channel_id=1, source_target_pairs={{0,1},{1,0},{2,3},{3,2},{4,5},{5,4},{6,7},{7,6},{8,9},{9,8},{10,11... | collective-permute-start | bytes 6291464 | tf_op jit(solution)/shard_map/ppermute | solution.py:392
  33.6 14.3 %collective-permute-start.2 = (bf16[128,1024]{1,0:T(8,128)(2,1)S(1)}, bf16[128,1024]{1,0:T(8,128)(2,1)S(1)}, u32[]{:S(2)}, u32[]{:S(2)}) collective-permute-start(bf16[128,1024]{1,0:T(8,128)(2,1)S(1)} %constant_dynamic-update-slice_fusion.refs_0_), channel_id=1, source_target_pairs={{0,4},{1,5},{2,6},{3,7},{4,8},{5,9},{6,10},{7,11},{8,12},{9,13},{1... | collective-permute-start | bytes 786440 | tf_op jit(solution)/shard_map/ppermute | solution.py:405
  34.0 14.0 %collective-permute-start.3 = (bf16[128,1024]{1,0:T(8,128)(2,1)S(1)}, bf16[128,1024]{1,0:T(8,128)(2,1)S(1)}, u32[]{:S(2)}, u32[]{:S(2)}) collective-permute-start(bf16[128,1024]{1,0:T(8,128)(2,1)S(1)} %constant_dynamic-update-slice_fusion.refs_0_), channel_id=1, source_target_pairs={{0,8},{1,9},{2,10},{3,11},{4,12},{5,13},{6,14},{7,15},{8,0},{9,1},... | collective-permute-start | bytes 786440 | tf_op jit(solution)/shard_map/ppermute | solution.py:405
  34.6 13.7 %collective-permute-start.4 = (bf16[128,1024]{1,0:T(8,128)(2,1)S(1)}, bf16[128,1024]{1,0:T(8,128)(2,1)S(1)}, u32[]{:S(2)}, u32[]{:S(2)}) collective-permute-start(bf16[128,1024]{1,0:T(8,128)(2,1)S(1)} %constant_dynamic-update-slice_fusion.refs_0_), channel_id=1, source_target_pairs={{0,12},{1,13},{2,14},{3,15},{4,0},{5,1},{6,2},{7,3},{8,4},{9,5},{1... | collective-permute-start | bytes 786440 | tf_op jit(solution)/shard_map/ppermute | solution.py:405
  48.0 0.7 copy-start.11
  48.0 0.8 copy-start.12
  48.4 0.7 copy-start.13
  49.1 6.0 %copy-start.14 = (s32[2048]{0:T(1024)S(1)}, s32[2048]{0:T(1024)}, u32[]{:S(2)}) copy-start(s32[2048]{0:T(1024)} %param.19) | copy-start | bytes 24580
  49.1 6.4 %copy-start.16 = (s32[4]{0:T(128)S(1)}, s32[4]{0:T(128)}, u32[]{:S(2)}) copy-start(s32[4]{0:T(128)} %param.21) | copy-start | bytes 52
  49.1 6.6 %copy-start.9 = (f32[64,64]{1,0:T(8,128)S(1)}, f32[64,64]{1,0:T(8,128)}, u32[]{:S(2)}) copy-start(f32[64,64]{1,0:T(8,128)} %table_ref.1) | copy-start | bytes 49156
  49.1 8.2 %copy-start.15 = (s32[4096]{0:T(1024)S(1)}, s32[4096]{0:T(1024)}, u32[]{:S(2)}) copy-start(s32[4096]{0:T(1024)} %param.20) | copy-start | bytes 49156
  49.1 22.5 %copy-start = (bf16[1,1024,1024]{2,1,0:T(8,128)(2,1)S(1)}, bf16[1,1024,1024]{2,1,0:T(8,128)(2,1)}, u32[]{:S(2)}) copy-start(bf16[1,1024,1024]{2,1,0:T(8,128)(2,1)} %get-tuple-element.22.refs_2_) | copy-start | bytes 6291460
  53.5 19.4 %collective-permute-start.8 = (bf16[1024,512]{1,0:T(8,128)(2,1)}, bf16[1024,512]{1,0:T(8,128)(2,1)}, u32[]{:S(2)}, u32[]{:S(2)}) collective-permute-start(bf16[1024,512]{1,0:T(8,128)(2,1)} %rotate_turned.1.t0), channel_id=1, source_target_pairs={{0,1},{1,0},{2,3},{3,2},{4,5},{5,4},{6,7},{7,6},{8,9},{9,8},{10,11... | collective-permute-start | bytes 3145736 | tf_op jit(solution)/shard_map/ppermute | solution.py:392
  55.1 16.5 %collective-permute-start.10 = (bf16[256,1152]{1,0:T(8,128)(2,1)S(1)}, bf16[256,1152]{1,0:T(8,128)(2,1)S(1)}, u32[]{:S(2)}, u32[]{:S(2)}) collective-permute-start(bf16[256,1152]{1,0:T(8,128)(2,1)S(1)} %get-tuple-element.18.refs_1_.refs_0_.refs_2_), channel_id=1, source_target_pairs={{0,2},{1,3},{2,0},{3,1},{4,6},{5,7},{6,4},{7,5},{8,10},{9,11},{10,... | collective-permute-start | bytes 1769480 | tf_op jit(solution)/shard_map/ppermute | solution.py:395
  56.5 0.8 copy-start.6
  57.4 33.1 %collective-permute-start.9 = (bf16[256,1024]{1,0:T(8,128)(2,1)}, bf16[256,1024]{1,0:T(8,128)(2,1)S(1)}, u32[]{:S(2)}, u32[]{:S(2)}) collective-permute-start(bf16[256,1024]{1,0:T(8,128)(2,1)} %copy-done.4), channel_id=1, source_target_pairs={{0,2},{1,3},{2,0},{3,1},{4,6},{5,7},{6,4},{7,5},{8,10},{9,11},{10,... | collective-permute-start | bytes 1572872 | tf_op jit(solution)/shard_map/ppermute | solution.py:395
  71.5 1.4 copy-start.2
  71.5 1.4 %copy-start.7 = (bf16[2048,128]{1,0:T(8,128)(2,1)S(1)}, bf16[2048,128]{1,0:T(8,128)(2,1)}, u32[]{:S(2)}) copy-start(bf16[2048,128]{1,0:T(8,128)(2,1)} %copy-done.6) | copy-start | bytes 1572868
  71.5 2.1 %copy-start.10 = (bf16[2,512,1024]{2,1,0:T(8,128)(2,1)S(1)}, bf16[2,512,1024]{2,1,0:T(8,128)(2,1)}, u32[]{:S(2)}) copy-start(bf16[2,512,1024]{2,1,0:T(8,128)(2,1)} %get-tuple-element.24.g0) | copy-start | bytes 6291460
  73.6 16.9 %copy-start.1 = (bf16[1,1024,1024]{2,1,0:T(8,128)(2,1)S(1)}, bf16[1,1024,1024]{2,1,0:T(8,128)(2,1)}, u32[]{:S(2)}) copy-start(bf16[1,1024,1024]{2,1,0:T(8,128)(2,1)} %get-tuple-element.21.refs_4_) | copy-start | bytes 6291460
  73.6 16.9 %copy-start.5 = (bf16[256,1024]{1,0:T(8,128)(2,1)S(1)}, bf16[256,1024]{1,0:T(8,128)(2,1)}, u32[]{:S(2)}) copy-start(bf16[256,1024]{1,0:T(8,128)(2,1)} %copy-done.4) | copy-start | bytes 1572868
  109.9 10.2 %all-to-all-start = ((f32[8,2,1024]{2,1,0:T(2,128)}), f32[8,2,1024]{2,1,0:T(2,128)S(1)}, u32[]{:S(2)}, u32[]{:S(2)}) async-start(f32[8,2,1024]{2,1,0:T(2,128)} %broadcast_in_dim.23), calls=%async_computation | async-start | bytes 131072 | tf_op jit(solution)/shard_map/all_to_all | solution.py:471
  120.2 15.2 %collective-permute-start.13 = (f32[2,512]{1,0:T(2,128)S(1)}, f32[2,512]{1,0:T(2,128)S(1)}, u32[]{:S(2)}, u32[]{:S(2)}) collective-permute-start(f32[2,512]{1,0:T(2,128)S(1)} %slice.9), channel_id=1, source_target_pairs={{0,1},{1,0},{2,3},{3,2},{4,5},{5,4},{6,7},{7,6},{8,9},{9,8},{10,11... | collective-permute-start | bytes 12296 | tf_op jit(solution)/shard_map/ppermute | solution.py:392
